TPU v7x, 256 devices: a whole 4x4x8 slice. The times are simulated.
256 devices in a mesh: sub: 32 (over y, z_hi, core), rng: 8 (over z_lo, x).
Axes of the slice: x: 4, y: 4, z: 8 (z_hi: 4, z_lo: 2; z = z_hi * 2 + z_lo), core: 2. Of those that a mesh axis runs over, the one named last changes fastest.
Arguments:
- image: bfloat16 [2, 8192, 4096], P(None, 'sub', 'rng'), may hold values from -30 to 30
- stencil: int32 [4, 2, 2, 256, 4], replicated, may hold values from 0 to 255, as said below
- interp_weights: float32 [4, 4], replicated, may hold values from 0.25 to 0.6
- range_taps: float32 [4, 2, 3], replicated, may hold values from 0.25 to 0.7
Outputs:
- merged: bfloat16 [2, 8192, 4096], P(None, 'sub', 'rng')
- beam_phase: float32 [2, 8192], P(None, 'sub')
Inputs may be any that keep to these rules, and one draw needn't show every extreme that they name: `stencil`: for every section, half, child and beam the 4 indices are consecutive and rising.
All inputs are finite; a program needn't handle non-finite values.
Results may differ from a plain program's by a relative error of at most 0.012.
Values may be sent and summed in bfloat16 or wider, within the bound.
A program may use at most 64 MiB of HBM per device.

v0:
```python
import jax
import jax.numpy as jnp
from jax import lax
from jax.sharding import Mesh
from jax.sharding import PartitionSpec as P

SECTIONS = 4
RNG = ("rng_0", "rng_1")


epsilon = 1e-06


def partner(value, axis, stride):
    mask = 2**stride
    pairs = [(source, source ^ mask) for source in range(lax.axis_size(axis))]
    return lax.ppermute(value, axis, pairs)


def with_halo(array, sides, width):
    for axis, dim in sides:
        size, length = (lax.axis_size(axis), array.shape[dim])
        up = [(i, (i + 1) % size) for i in range(size - 1)]
        down = [(j, i) for i, j in up]
        last = lax.slice_in_dim(array, length - width, length, axis=dim)
        initial = lax.slice_in_dim(array, 0, width, axis=dim)
        before = lax.ppermute(last, axis, up)
        after = lax.ppermute(initial, axis, down)
        array = jnp.concatenate([before, array, after], axis=dim)
    return array


def by_axis(array, axes):
    for axis in axes:
        array = lax.psum(array, axis)
    return array


def coefficients(weights, section_num, beams_dev):
    beam_pos = jnp.arange(beams_dev, dtype=jnp.float32)
    half_pos = jnp.arange(2, dtype=jnp.float32).reshape(2, 1, 1)
    child_sign = (2.0 * jnp.arange(2, dtype=jnp.float32) - 1.0).reshape(1, 2, 1)
    angles = child_sign * (half_pos * beams_dev + beam_pos + 0.5) * (0.37 + 0.11 * section_num)
    real_part = (jnp.cos(angles)[..., None] * weights).astype(jnp.bfloat16)
    imag_part = (jnp.sin(angles)[..., None] * weights).astype(jnp.bfloat16)
    return (real_part, imag_part)


def rotate_rows(blocks, factors):
    values = blocks.astype(jnp.float32)
    real_factor = factors[0][..., None]
    imag_factor = factors[1][..., None]
    real_out = values[0] * real_factor - values[1] * imag_factor
    imag_out = values[0] * imag_factor + values[1] * real_factor
    return jnp.stack([real_out, imag_out]).astype(jnp.bfloat16)


def pick_entry(table, half_bit, child_bit):
    inner = lax.dynamic_index_in_dim(table, half_bit, 0, keepdims=False)
    return lax.dynamic_index_in_dim(inner, child_bit, 0, keepdims=False)


def build_matrix(table, real_part, imag_part, half_bit, child_bit, columns):
    indices = pick_entry(table, half_bit, child_bit)
    coef_re = pick_entry(real_part, half_bit, child_bit).astype(jnp.float32)
    coef_im = pick_entry(imag_part, half_bit, child_bit).astype(jnp.float32)
    onehot = (indices[:, :, None] == columns[None, None, :]).astype(jnp.float32)
    matrix_re = jnp.einsum("at,atc->ac", coef_re, onehot).astype(jnp.bfloat16)
    matrix_im = jnp.einsum("at,atc->ac", coef_im, onehot).astype(jnp.bfloat16)
    return (matrix_re, matrix_im)


def complex_apply(matrices, block):
    matrix_re, matrix_im = matrices
    real_out = jnp.dot(matrix_re, block[0], preferred_element_type=jnp.float32) - jnp.dot(
        matrix_im, block[1], preferred_element_type=jnp.float32
    )
    imag_out = jnp.dot(matrix_re, block[1], preferred_element_type=jnp.float32) + jnp.dot(
        matrix_im, block[0], preferred_element_type=jnp.float32
    )
    return jnp.stack([real_out, imag_out])


def local_sums(merged):
    values = merged.astype(jnp.float32)
    following = jnp.roll(values, -1, axis=1)
    lag_real = jnp.sum(values[0] * following[0] + values[1] * following[1], axis=-1)
    lag_imag = jnp.sum(values[0] * following[1] - values[1] * following[0], axis=-1)
    power = jnp.sum(
        (values[0] ** 2 + values[1] ** 2) * (following[0] ** 2 + following[1] ** 2), axis=-1
    )
    return (lag_real, lag_imag, power)


def on_device(image, stencil, interp_weights, range_taps):
    beams_dev = image.shape[1]
    sub_index = lax.axis_index("sub")
    columns = jnp.arange(beams_dev, dtype=jnp.int32)
    merged = image
    factors = None
    for section_num in range(SECTIONS):
        span = 2**section_num
        half_bit = sub_index // span % 2
        other_bit = 1 - half_bit
        real_part, imag_part = coefficients(interp_weights[section_num], section_num, beams_dev)
        table = stencil[section_num]
        partner_raw = partner(merged, "sub", section_num)
        if section_num == 0:
            own_block = merged
            partner_block = partner_raw
        else:
            partner_factors = partner(factors, "sub", section_num)
            own_block = rotate_rows(merged, factors)
            partner_block = rotate_rows(partner_raw, partner_factors)
        own_terms = complex_apply(
            build_matrix(table, real_part, imag_part, half_bit, half_bit, columns), own_block
        )
        partner_terms = complex_apply(
            build_matrix(table, real_part, imag_part, half_bit, other_bit, columns), partner_block
        )
        taps_own = lax.dynamic_index_in_dim(range_taps[section_num], half_bit, 0, keepdims=False)
        taps_partner = lax.dynamic_index_in_dim(
            range_taps[section_num], other_bit, 0, keepdims=False
        )
        lower_terms = taps_own[0] * own_terms + taps_partner[0] * partner_terms
        middle_terms = taps_own[1] * own_terms + taps_partner[1] * partner_terms
        upper_terms = taps_own[2] * own_terms + taps_partner[2] * partner_terms
        edges = jnp.stack([upper_terms[:, :, 0], lower_terms[:, :, -1]], axis=-1)
        rims = with_halo(edges, ((RNG, 2),), 1)
        shifted_lower = jnp.concatenate([rims[:, :, 0:1], lower_terms[:, :, :-1]], axis=-1)
        shifted_upper = jnp.concatenate([upper_terms[:, :, 1:], rims[:, :, 3:4]], axis=-1)
        merged = (middle_terms + shifted_lower + shifted_upper).astype(jnp.bfloat16)
        lag_real, lag_imag, power = jax.tree.map(
            lambda part: by_axis(part, RNG), local_sums(merged)
        )
        scale = 1.0 / jnp.sqrt(power + epsilon)
        factors = jnp.stack([lag_real * scale, -lag_imag * scale])
    return (merged, factors)


def solution(mesh):
    torus = Mesh(mesh.devices.reshape(mesh.shape["sub"], 2, 4), ("sub", "rng_0", "rng_1"))
    placed = (P(None, "sub", RNG), P(), P(), P())
    return jax.shard_map(
        on_device,
        mesh=torus,
        in_specs=placed,
        out_specs=(P(None, "sub", RNG), P(None, "sub")),
        check_vma=False,
    )
```

profile of v0, /device:TPU:16, one launch (start us, length us, event | category | flops | bytes accessed | tf_op | source)
XLA Modules:
  0.0 227.7 jit_solution(9777337125828858418)
XLA Ops:
  2.4 1.4 fusion.33
  4.3 1.4 fusion.32
  6.3 2.0 fusion.30
  8.4 2.0 fusion.31
  11.0 2.0 fusion.35
  13.0 2.0 fusion.34
  15.1 2.0 fusion.29
  17.2 2.0 fusion.28
  20.0 2.0 fusion.37
  22.0 2.0 fusion.36
  24.8 2.0 fusion.27
  28.2 2.0 fusion.26
  30.3 1.4 fusion.39
  33.9 2.7 %multiply_add_fusion.7 = (f32[2,256,512]{2,1,0:T(8,128)S(1)}, f32[2,256,512]{2,1,0:T(8,128)S(1)}) fusion(f32[1,256,512]{2,1,0:T(8,128)S(1)} %fusion.12, f32[1,256,512]{2,1,0:T(8,128)S(1)} %fusion.13, f32[1,256,512]{2,1,0:T(8,128)S(1)} %fusion.14, f32[1,256,512]{2,1,0:T(8,128)S(1)} %fusion.15, f32[]{:T(128)} %bitcast.44, f32[]{:T(128)} %bitcast.43, ...), kind=kLoop, calls=%fused_computation.76 | loop fusion | flops 2097152 | bytes 4194320 | tf_op jit(solution)/shard_map/add | solution.py:125
  36.8 4.1 %collective-permute-start.1 = (f32[2,256,1]{2,1,0:T(8,128)S(1)}, f32[2,256,1]{2,1,0:T(8,128)}, u32[]{:S(2)}, u32[]{:S(2)}) collective-permute-start(f32[2,256,1]{2,1,0:T(8,128)S(1)} %slice.532), channel_id=1, source_target_pairs={{0,1},{1,2},{2,3},{3,4},{4,5},{5,6},{6,7},{8,9},{9,10},{10,11},{11... | collective-permute-start | bytes 6152 | tf_op jit(solution)/shard_map/ppermute | solution.py:27
  42.3 2.2 fusion.38
  45.0 1.4 collective-permute-done.1
  46.4 5.0 %collective-permute-done.2 = f32[2,256,1]{2,1,0:T(8,128)} collective-permute-done((f32[2,256,1]{2,1,0:T(8,128)S(1)}, f32[2,256,1]{2,1,0:T(8,128)}, u32[]{:S(2)}, u32[]{:S(2)}) %collective-permute-start.2) | collective-permute-done | bytes 2080 | tf_op jit(solution)/shard_map/ppermute | solution.py:28
  51.3 2.9 %fusion.138 = (f32[2,256,512]{2,1,0:T(8,128)S(1)}, bf16[2,256,512]{2,1,0:T(8,128)(2,1)S(1)}) fusion(f32[2,256,1]{2,1,0:T(8,128)} %collective-permute-done.2, f32[2,256,511]{2,1,0:T(8,128)S(1)} %slice.534, f32[2,256,511]{2,1,0:T(8,128)S(1)} %bitcast.293, f32[2,256,1]{2,1,0:T(8,128)} %collective-permute-done.1, f32[1,256,512]{2,1,0:T(8,128)S(1)} %copy-done.6, ...), kind=kLoop, calls=%fused_computation.312 | loop fusion | flops 2883584 | bytes 5767176 | tf_op jit(solution)/shard_map/convert_element_type | solution.py:50
  54.4 3.4 %collective-permute-start.3 = (bf16[2,256,512]{2,1,0:T(8,128)(2,1)S(1)}, bf16[2,256,512]{2,1,0:T(8,128)(2,1)S(1)}, u32[]{:S(2)}, u32[]{:S(2)}) collective-permute-start(bf16[2,256,512]{2,1,0:T(8,128)(2,1)S(1)} %get-tuple-element.45), channel_id=1, source_target_pairs={{0,16},{8,24},{16,0},{24,8},{32,48},{40,56},{48,32},{56,40},{64,80... | collective-permute-start | bytes 1572872 | tf_op jit(solution)/shard_map/ppermute | solution.py:17
  59.4 9.2 %all-reduce.7 = (f32[256]{0:T(256)S(1)}, f32[256]{0:T(256)S(1)}, f32[256]{0:T(256)S(1)}) all-reduce(f32[256]{0:T(256)S(1)} %copy-done.25, f32[256]{0:T(256)S(1)} %get-tuple-element.12, f32[256]{0:T(256)S(1)} %get-tuple-element.11), channel_id=1, replica_groups=mesh['sub'=32,'rng_0'=2,'rng_1'=4] {'rng_0'}, use_global_device_ids=true, to_apply=%region_7.8 | all-reduce | flops 768 | bytes 6144 | tf_op jit(solution)/shard_map/psum | solution.py:35
  68.6 12.2 %all-reduce.3 = (f32[256]{0:T(256)S(1)}, f32[256]{0:T(256)S(1)}, f32[256]{0:T(256)S(1)}) all-reduce(f32[256]{0:T(256)S(1)} %get-tuple-element.35, f32[256]{0:T(256)S(1)} %get-tuple-element.36, f32[256]{0:T(256)S(1)} %get-tuple-element.37), channel_id=1, replica_groups=mesh['sub'=32,'rng_0'=2,'rng_1'=4] {'rng_1'}, use_global_device_ids=true, to_apply=%region_8.9 | all-reduce | flops 768 | bytes 6144 | tf_op jit(solution)/shard_map/psum | solution.py:35
  83.4 3.4 %collective-permute-done.4 = f32[2,256]{1,0:T(2,128)S(1)} collective-permute-done((f32[2,256]{1,0:T(2,128)S(1)}, f32[2,256]{1,0:T(2,128)S(1)}, u32[]{:S(2)}, u32[]{:S(2)}) %collective-permute-start.4) | collective-permute-done | bytes 2080 | tf_op jit(solution)/shard_map/ppermute | solution.py:17
  89.6 2.8 %multiply_add_fusion.5 = (f32[2,256,512]{2,1,0:T(8,128)S(1)}, f32[2,256,512]{2,1,0:T(8,128)S(1)}) fusion(f32[1,256,512]{2,1,0:T(8,128)S(1)} %fusion.8, f32[1,256,512]{2,1,0:T(8,128)S(1)} %fusion.9, f32[1,256,512]{2,1,0:T(8,128)S(1)} %fusion.10, f32[1,256,512]{2,1,0:T(8,128)S(1)} %fusion.11, f32[]{:T(128)} %bitcast.71, f32[]{:T(128)} %bitcast.70, ...), kind=kLoop, calls=%fused_computation.71 | loop fusion | flops 2097152 | bytes 4194320 | tf_op jit(solution)/shard_map/add | solution.py:125
  92.5 1.3 collective-permute-start.5
  95.2 1.4 fusion.25
  97.7 4.5 %collective-permute-done.6 = f32[2,256,1]{2,1,0:T(8,128)S(1)} collective-permute-done((f32[2,256,1]{2,1,0:T(8,128)S(1)}, f32[2,256,1]{2,1,0:T(8,128)S(1)}, u32[]{:S(2)}, u32[]{:S(2)}) %collective-permute-start.6) | collective-permute-done | bytes 2080 | tf_op jit(solution)/shard_map/ppermute | solution.py:28
  102.2 1.9 fusion.136
  104.2 4.6 %collective-permute-start.7 = (bf16[2,256,512]{2,1,0:T(8,128)(2,1)S(1)}, bf16[2,256,512]{2,1,0:T(8,128)(2,1)S(1)}, u32[]{:S(2)}, u32[]{:S(2)}) collective-permute-start(bf16[2,256,512]{2,1,0:T(8,128)(2,1)S(1)} %get-tuple-element.43), channel_id=1, source_target_pairs={{0,32},{8,40},{16,48},{24,56},{32,0},{40,8},{48,16},{56,24},{64,96... | collective-permute-start | bytes 1572872 | tf_op jit(solution)/shard_map/ppermute | solution.py:17
  109.3 21.4 %all-reduce.6 = (f32[256]{0:T(256)S(1)}, f32[256]{0:T(256)S(1)}, f32[256]{0:T(256)S(1)}) all-reduce(f32[256]{0:T(256)S(1)} %get-tuple-element.10, f32[256]{0:T(256)S(1)} %get-tuple-element.9, f32[256]{0:T(256)S(1)} %get-tuple-element.8), channel_id=1, replica_groups=mesh['sub'=32,'rng_0'=2,'rng_1'=4] {'rng_0'}, use_global_device_ids=true, to_apply=%region_16.17 | all-reduce | flops 768 | bytes 6144 | tf_op jit(solution)/shard_map/psum | solution.py:35
  130.7 10.4 %all-reduce.2 = (f32[256]{0:T(256)S(1)}, f32[256]{0:T(256)S(1)}, f32[256]{0:T(256)S(1)}) all-reduce(f32[256]{0:T(256)S(1)} %get-tuple-element.32, f32[256]{0:T(256)S(1)} %get-tuple-element.33, f32[256]{0:T(256)S(1)} %get-tuple-element.34), channel_id=1, replica_groups=mesh['sub'=32,'rng_0'=2,'rng_1'=4] {'rng_1'}, use_global_device_ids=true, to_apply=%region_17.18 | all-reduce | flops 768 | bytes 6144 | tf_op jit(solution)/shard_map/psum | solution.py:35
  142.5 3.2 %collective-permute-start.8 = (f32[2,256]{1,0:T(2,128)S(1)}, f32[2,256]{1,0:T(2,128)S(1)}, u32[]{:S(2)}, u32[]{:S(2)}) collective-permute-start(f32[2,256]{1,0:T(2,128)S(1)} %pad_maximum_fusion.13), channel_id=1, source_target_pairs={{0,32},{8,40},{16,48},{24,56},{32,0},{40,8},{48,16},{56,24},{64,96... | collective-permute-start | bytes 6152 | tf_op jit(solution)/shard_map/ppermute | solution.py:17
  146.2 3.9 %collective-permute-done.8 = f32[2,256]{1,0:T(2,128)S(1)} collective-permute-done((f32[2,256]{1,0:T(2,128)S(1)}, f32[2,256]{1,0:T(2,128)S(1)}, u32[]{:S(2)}, u32[]{:S(2)}) %collective-permute-start.8) | collective-permute-done | bytes 2080 | tf_op jit(solution)/shard_map/ppermute | solution.py:17
  152.8 2.8 %multiply_add_fusion.3 = (f32[2,256,512]{2,1,0:T(8,128)S(1)}, f32[2,256,512]{2,1,0:T(8,128)S(1)}) fusion(f32[1,256,512]{2,1,0:T(8,128)S(1)} %fusion.4, f32[1,256,512]{2,1,0:T(8,128)S(1)} %fusion.5, f32[1,256,512]{2,1,0:T(8,128)S(1)} %fusion.6, f32[1,256,512]{2,1,0:T(8,128)S(1)} %fusion.7, f32[]{:T(128)} %bitcast.98, f32[]{:T(128)} %bitcast.97, f32[]{:T(128)} %bitcast.100, ...), kind=kLoop, calls=%fused_computation.66 | loop fusion | flops 2097152 | bytes 4194320 | tf_op jit(solution)/shard_map/add | solution.py:125
  157.1 4.6 %collective-permute-start.9 = (f32[2,256,1]{2,1,0:T(8,128)S(1)}, f32[2,256,1]{2,1,0:T(8,128)S(1)}, u32[]{:S(2)}, u32[]{:S(2)}) collective-permute-start(f32[2,256,1]{2,1,0:T(8,128)S(1)} %slice.560), channel_id=1, source_target_pairs={{0,1},{1,2},{2,3},{3,4},{4,5},{5,6},{6,7},{8,9},{9,10},{10,11},{11... | collective-permute-start | bytes 6152 | tf_op jit(solution)/shard_map/ppermute | solution.py:27
  161.7 2.3 fusion.24
  165.5 1.8 fusion.134
  167.5 1.4 collective-permute-start.11
  169.4 8.0 %all-reduce.5 = (f32[256]{0:T(256)S(1)}, f32[256]{0:T(256)S(1)}, f32[256]{0:T(256)S(1)}) all-reduce(f32[256]{0:T(256)S(1)} %get-tuple-element.7, f32[256]{0:T(256)S(1)} %get-tuple-element.6, f32[256]{0:T(256)S(1)} %get-tuple-element.5), channel_id=1, replica_groups=mesh['sub'=32,'rng_0'=2,'rng_1'=4] {'rng_0'}, use_global_device_ids=true, to_apply=%region_25.26 | all-reduce | flops 768 | bytes 6144 | tf_op jit(solution)/shard_map/psum | solution.py:35
  177.3 7.8 %all-reduce.1 = (f32[256]{0:T(256)S(1)}, f32[256]{0:T(256)S(1)}, f32[256]{0:T(256)S(1)}) all-reduce(f32[256]{0:T(256)S(1)} %get-tuple-element.29, f32[256]{0:T(256)S(1)} %get-tuple-element.30, f32[256]{0:T(256)S(1)} %get-tuple-element.31), channel_id=1, replica_groups=mesh['sub'=32,'rng_0'=2,'rng_1'=4] {'rng_1'}, use_global_device_ids=true, to_apply=%region_26.27 | all-reduce | flops 768 | bytes 6144 | tf_op jit(solution)/shard_map/psum | solution.py:35
  187.1 2.4 %collective-permute-done.12 = f32[2,256]{1,0:T(2,128)S(1)} collective-permute-done((f32[2,256]{1,0:T(2,128)S(1)}, f32[2,256]{1,0:T(2,128)S(1)}, u32[]{:S(2)}, u32[]{:S(2)}) %collective-permute-start.12) | collective-permute-done | bytes 2080 | tf_op jit(solution)/shard_map/ppermute | solution.py:17
  191.5 2.7 %multiply_add_fusion.1 = (f32[2,256,512]{2,1,0:T(8,128)S(1)}, f32[2,256,512]{2,1,0:T(8,128)S(1)}) fusion(f32[1,256,512]{2,1,0:T(8,128)S(1)} %fusion, f32[1,256,512]{2,1,0:T(8,128)S(1)} %fusion.1, f32[1,256,512]{2,1,0:T(8,128)S(1)} %fusion.2, f32[1,256,512]{2,1,0:T(8,128)S(1)} %fusion.3, f32[]{:T(128)} %bitcast.125, f32[]{:T(128)} %bitcast.124, f32[]{:T(128)} %bitcast.127, ...), kind=kLoop, calls=%fused_computation.61 | loop fusion | flops 2097152 | bytes 4194320 | tf_op jit(solution)/shard_map/add | solution.py:125
  194.4 3.9 %collective-permute-start.13 = (f32[2,256,1]{2,1,0:T(8,128)S(1)}, f32[2,256,1]{2,1,0:T(8,128)S(1)}, u32[]{:S(2)}, u32[]{:S(2)}) collective-permute-start(f32[2,256,1]{2,1,0:T(8,128)S(1)} %slice.574), channel_id=1, source_target_pairs={{0,1},{1,2},{2,3},{3,4},{4,5},{5,6},{6,7},{8,9},{9,10},{10,11},{11... | collective-permute-start | bytes 6152 | tf_op jit(solution)/shard_map/ppermute | solution.py:27
  199.9 2.2 collective-permute-done.13
  202.1 4.5 %collective-permute-done.14 = f32[2,256,1]{2,1,0:T(8,128)S(1)} collective-permute-done((f32[2,256,1]{2,1,0:T(8,128)S(1)}, f32[2,256,1]{2,1,0:T(8,128)S(1)}, u32[]{:S(2)}, u32[]{:S(2)}) %collective-permute-start.14) | collective-permute-done | bytes 2080 | tf_op jit(solution)/shard_map/ppermute | solution.py:28
  206.6 1.9 fusion.132
  209.7 4.9 %all-reduce.4 = (f32[256]{0:T(256)S(1)}, f32[256]{0:T(256)S(1)}, f32[256]{0:T(256)S(1)}) all-reduce(f32[256]{0:T(256)S(1)} %get-tuple-element.4, f32[256]{0:T(256)S(1)} %get-tuple-element.3, f32[256]{0:T(256)S(1)} %get-tuple-element.2), channel_id=1, replica_groups=mesh['sub'=32,'rng_0'=2,'rng_1'=4] {'rng_0'}, use_global_device_ids=true, to_apply=%region_34.35 | all-reduce | flops 768 | bytes 6144 | tf_op jit(solution)/shard_map/psum | solution.py:35
  214.7 12.5 %all-reduce = (f32[256]{0:T(256)S(1)}, f32[256]{0:T(256)S(1)}, f32[256]{0:T(256)S(1)}) all-reduce(f32[256]{0:T(256)S(1)} %get-tuple-element.26, f32[256]{0:T(256)S(1)} %get-tuple-element.27, f32[256]{0:T(256)S(1)} %get-tuple-element.28), channel_id=1, replica_groups=mesh['sub'=32,'rng_0'=2,'rng_1'=4] {'rng_1'}, use_global_device_ids=true, to_apply=%region_35.36 | all-reduce | flops 768 | bytes 6144 | tf_op jit(solution)/shard_map/psum | solution.py:35
  (172 shorter events, 36.6 us)
Async XLA Ops:
  0.6 0.9 copy-start.20
  0.6 31.0 %collective-permute-start = (bf16[2,256,512]{2,1,0:T(8,128)(2,1)}, bf16[2,256,512]{2,1,0:T(8,128)(2,1)S(1)}, u32[]{:S(2)}, u32[]{:S(2)}) collective-permute-start(bf16[2,256,512]{2,1,0:T(8,128)(2,1)} %param.4), channel_id=1, source_target_pairs={{0,8},{8,0},{16,24},{24,16},{32,40},{40,32},{48,56},{56,48},{64,72... | collective-permute-start | bytes 1572872 | tf_op jit(solution)/shard_map/ppermute | solution.py:17
  0.8 0.7 copy-start.26
  2.4 1.4 copy-start.7
  6.2 27.1 %copy-start.1 = (f32[1,256,512]{2,1,0:T(8,128)}, f32[1,256,512]{2,1,0:T(8,128)S(1)}, u32[]{:S(2)}) copy-start(f32[1,256,512]{2,1,0:T(8,128)S(1)} %fusion.14) | copy-start | bytes 1572868
  8.4 2.0 copy-start.24
  30.3 1.4 copy-start.12
  31.9 1.0 copy-start.18
  33.1 0.8 copy-start.3
  33.3 3.3 %copy-start.5 = (f32[1,256,512]{2,1,0:T(8,128)}, f32[1,256,512]{2,1,0:T(8,128)S(1)}, u32[]{:S(2)}) copy-start(f32[1,256,512]{2,1,0:T(8,128)S(1)} %fusion.12) | copy-start | bytes 1572868
  36.8 9.6 %collective-permute-start.1 = (f32[2,256,1]{2,1,0:T(8,128)S(1)}, f32[2,256,1]{2,1,0:T(8,128)}, u32[]{:S(2)}, u32[]{:S(2)}) collective-permute-start(f32[2,256,1]{2,1,0:T(8,128)S(1)} %slice.532), channel_id=1, source_target_pairs={{0,1},{1,2},{2,3},{3,4},{4,5},{5,6},{6,7},{8,9},{9,10},{10,11},{11... | collective-permute-start | bytes 6152 | tf_op jit(solution)/shard_map/ppermute | solution.py:27
  40.9 1.3 copy-start.23
  40.9 10.4 %collective-permute-start.2 = (f32[2,256,1]{2,1,0:T(8,128)S(1)}, f32[2,256,1]{2,1,0:T(8,128)}, u32[]{:S(2)}, u32[]{:S(2)}) collective-permute-start(f32[2,256,1]{2,1,0:T(8,128)S(1)} %slice.535), channel_id=1, source_target_pairs={{1,0},{2,1},{3,2},{4,3},{5,4},{6,5},{7,6},{9,8},{10,9},{11,10},{12... | collective-permute-start | bytes 6152 | tf_op jit(solution)/shard_map/ppermute | solution.py:28
  44.6 6.7 %copy-start.2 = (f32[1,256,512]{2,1,0:T(8,128)S(1)}, f32[1,256,512]{2,1,0:T(8,128)}, u32[]{:S(2)}) copy-start(f32[1,256,512]{2,1,0:T(8,128)} %copy-done.1) | copy-start | bytes 1572868
  44.6 6.7 %copy-start.4 = (f32[1,256,512]{2,1,0:T(8,128)S(1)}, f32[1,256,512]{2,1,0:T(8,128)}, u32[]{:S(2)}) copy-start(f32[1,256,512]{2,1,0:T(8,128)} %copy-done.3) | copy-start | bytes 1572868
  44.6 6.7 %copy-start.6 = (f32[1,256,512]{2,1,0:T(8,128)S(1)}, f32[1,256,512]{2,1,0:T(8,128)}, u32[]{:S(2)}) copy-start(f32[1,256,512]{2,1,0:T(8,128)} %copy-done.5) | copy-start | bytes 1572868
  54.4 32.4 %collective-permute-start.3 = (bf16[2,256,512]{2,1,0:T(8,128)(2,1)S(1)}, bf16[2,256,512]{2,1,0:T(8,128)(2,1)S(1)}, u32[]{:S(2)}, u32[]{:S(2)}) collective-permute-start(bf16[2,256,512]{2,1,0:T(8,128)(2,1)S(1)} %get-tuple-element.45), channel_id=1, source_target_pairs={{0,16},{8,24},{16,0},{24,8},{32,48},{40,56},{48,32},{56,40},{64,80... | collective-permute-start | bytes 1572872 | tf_op jit(solution)/shard_map/ppermute | solution.py:17
  58.7 0.7 copy-start.25
  80.8 1.0 copy-start.11
  82.0 1.0 copy-start.17
  82.2 4.6 %collective-permute-start.4 = (f32[2,256]{1,0:T(2,128)S(1)}, f32[2,256]{1,0:T(2,128)S(1)}, u32[]{:S(2)}, u32[]{:S(2)}) collective-permute-start(f32[2,256]{1,0:T(2,128)S(1)} %pad_maximum_fusion.12), channel_id=1, source_target_pairs={{0,16},{8,24},{16,0},{24,8},{32,48},{40,56},{48,32},{56,40},{64,80... | collective-permute-start | bytes 6152 | tf_op jit(solution)/shard_map/ppermute | solution.py:17
  86.9 1.0 copy-start.10
  88.1 1.0 copy-start.16
  92.5 5.2 %collective-permute-start.5 = (f32[2,256,1]{2,1,0:T(8,128)S(1)}, f32[2,256,1]{2,1,0:T(8,128)S(1)}, u32[]{:S(2)}, u32[]{:S(2)}) collective-permute-start(f32[2,256,1]{2,1,0:T(8,128)S(1)} %slice.546), channel_id=1, source_target_pairs={{0,1},{1,2},{2,3},{3,4},{4,5},{5,6},{6,7},{8,9},{9,10},{10,11},{11... | collective-permute-start | bytes 6152 | tf_op jit(solution)/shard_map/ppermute | solution.py:27
  93.9 1.4 copy-start.22
  93.9 8.3 %collective-permute-start.6 = (f32[2,256,1]{2,1,0:T(8,128)S(1)}, f32[2,256,1]{2,1,0:T(8,128)S(1)}, u32[]{:S(2)}, u32[]{:S(2)}) collective-permute-start(f32[2,256,1]{2,1,0:T(8,128)S(1)} %slice.549), channel_id=1, source_target_pairs={{1,0},{2,1},{3,2},{4,3},{5,4},{6,5},{7,6},{9,8},{10,9},{11,10},{12... | collective-permute-start | bytes 6152 | tf_op jit(solution)/shard_map/ppermute | solution.py:28
  104.2 45.9 %collective-permute-start.7 = (bf16[2,256,512]{2,1,0:T(8,128)(2,1)S(1)}, bf16[2,256,512]{2,1,0:T(8,128)(2,1)S(1)}, u32[]{:S(2)}, u32[]{:S(2)}) collective-permute-start(bf16[2,256,512]{2,1,0:T(8,128)(2,1)S(1)} %get-tuple-element.43), channel_id=1, source_target_pairs={{0,32},{8,40},{16,48},{24,56},{32,0},{40,8},{48,16},{56,24},{64,96... | collective-permute-start | bytes 1572872 | tf_op jit(solution)/shard_map/ppermute | solution.py:17
  141.1 1.0 copy-start.9
  142.3 3.4 %copy-start.14 = (bf16[256,1,256]{2,1,0:T(2,128)(2,1)S(1)}, bf16[256,1,256]{2,1,0:T(2,128)(2,1)}, u32[]{:S(2)}) copy-start(bf16[256,1,256]{2,1,0:T(2,128)(2,1)} %fusion.36) | copy-start | bytes 393220
  142.5 7.6 %collective-permute-start.8 = (f32[2,256]{1,0:T(2,128)S(1)}, f32[2,256]{1,0:T(2,128)S(1)}, u32[]{:S(2)}, u32[]{:S(2)}) collective-permute-start(f32[2,256]{1,0:T(2,128)S(1)} %pad_maximum_fusion.13), channel_id=1, source_target_pairs={{0,32},{8,40},{16,48},{24,56},{32,0},{40,8},{48,16},{56,24},{64,96... | collective-permute-start | bytes 6152 | tf_op jit(solution)/shard_map/ppermute | solution.py:17
  150.2 1.0 copy-start.8
  151.4 1.0 copy-start.15
  155.6 8.6 %collective-permute-start.10 = (f32[2,256,1]{2,1,0:T(8,128)S(1)}, f32[2,256,1]{2,1,0:T(8,128)S(1)}, u32[]{:S(2)}, u32[]{:S(2)}) collective-permute-start(f32[2,256,1]{2,1,0:T(8,128)S(1)} %slice.563), channel_id=1, source_target_pairs={{1,0},{2,1},{3,2},{4,3},{5,4},{6,5},{7,6},{9,8},{10,9},{11,10},{12... | collective-permute-start | bytes 6152 | tf_op jit(solution)/shard_map/ppermute | solution.py:28
  156.9 4.7 %copy-start.21 = (bf16[256,4,1]{1,0,2:T(8,128)(2,1)S(1)}, bf16[256,4,1]{1,0,2:T(8,128)(2,1)}, u32[]{:S(2)}) copy-start(bf16[256,4,1]{1,0,2:T(8,128)(2,1)} %get-tuple-element.67) | copy-start | bytes 6148
  157.1 8.4 %collective-permute-start.9 = (f32[2,256,1]{2,1,0:T(8,128)S(1)}, f32[2,256,1]{2,1,0:T(8,128)S(1)}, u32[]{:S(2)}, u32[]{:S(2)}) collective-permute-start(f32[2,256,1]{2,1,0:T(8,128)S(1)} %slice.560), channel_id=1, source_target_pairs={{0,1},{1,2},{2,3},{3,4},{4,5},{5,6},{6,7},{8,9},{9,10},{10,11},{11... | collective-permute-start | bytes 6152 | tf_op jit(solution)/shard_map/ppermute | solution.py:27
  167.5 22.0 %collective-permute-start.11 = (bf16[2,256,512]{2,1,0:T(8,128)(2,1)S(1)}, bf16[2,256,512]{2,1,0:T(8,128)(2,1)S(1)}, u32[]{:S(2)}, u32[]{:S(2)}) collective-permute-start(bf16[2,256,512]{2,1,0:T(8,128)(2,1)S(1)} %get-tuple-element.41), channel_id=1, source_target_pairs={{0,64},{8,72},{16,80},{24,88},{32,96},{40,104},{48,112},{56,120},{... | collective-permute-start | bytes 1572872 | tf_op jit(solution)/shard_map/ppermute | solution.py:17
  185.6 1.1 copy-start.13
  185.8 3.7 %collective-permute-start.12 = (f32[2,256]{1,0:T(2,128)S(1)}, f32[2,256]{1,0:T(2,128)S(1)}, u32[]{:S(2)}, u32[]{:S(2)}) collective-permute-start(f32[2,256]{1,0:T(2,128)S(1)} %pad_maximum_fusion.14), channel_id=1, source_target_pairs={{0,64},{8,72},{16,80},{24,88},{32,96},{40,104},{48,112},{56,120},{... | collective-permute-start | bytes 6152 | tf_op jit(solution)/shard_map/ppermute | solution.py:17
  190.1 1.0 copy-start.19
  194.4 7.7 %collective-permute-start.13 = (f32[2,256,1]{2,1,0:T(8,128)S(1)}, f32[2,256,1]{2,1,0:T(8,128)S(1)}, u32[]{:S(2)}, u32[]{:S(2)}) collective-permute-start(f32[2,256,1]{2,1,0:T(8,128)S(1)} %slice.574), channel_id=1, source_target_pairs={{0,1},{1,2},{2,3},{3,4},{4,5},{5,6},{6,7},{8,9},{9,10},{10,11},{11... | collective-permute-start | bytes 6152 | tf_op jit(solution)/shard_map/ppermute | solution.py:27
  198.3 8.3 %collective-permute-start.14 = (f32[2,256,1]{2,1,0:T(8,128)S(1)}, f32[2,256,1]{2,1,0:T(8,128)S(1)}, u32[]{:S(2)}, u32[]{:S(2)}) collective-permute-start(f32[2,256,1]{2,1,0:T(8,128)S(1)} %slice.577), channel_id=1, source_target_pairs={{1,0},{2,1},{3,2},{4,3},{5,4},{6,5},{7,6},{9,8},{10,9},{11,10},{12... | collective-permute-start | bytes 6152 | tf_op jit(solution)/shard_map/ppermute | solution.py:28
  208.4 0.8 copy-start
where the time goes:
time: 229 us; the launch traced here: 228 us
  blocking collectives  86.4 us (38%)
  matrix products  37.3 us (16%)
  starting transfers between devices  32.5 us (14%)
  waiting for transfers between devices  28.5 us (12%)
  other arithmetic  25.8 us (11%)
  local copies, waits for them, and re-layouts  15.5 us (7%)
    psum x8, blocking collectives, by_axis(): array = lax.psum(array, axis)  86.4 us
    dot_general x8, matrix products, build_matrix(): matrix_im = jnp.einsum('at,atc->ac', coef_im, onehot).astype(jnp.bfloat16)  15.9 us
    dot_general x8, matrix products, build_matrix(): matrix_re = jnp.einsum('at,atc->ac', coef_re, onehot).astype(jnp.bfloat16)  14.2 us
    ppermute x4, waiting for transfers between devices, with_halo(): after = lax.ppermute(initial, axis, down)  13.9 us
    ppermute x4, starting transfers between devices, with_halo(): before = lax.ppermute(last, axis, up)  13.8 us
    ppermute x7, starting transfers between devices, partner(): return lax.ppermute(value, axis, pairs)  13.5 us
    add x4, other arithmetic, on_device(): lower_terms = taps_own[0] * own_terms + taps_partner[0] * partner_terms  11 us
    ppermute x7, waiting for transfers between devices, partner(): return lax.ppermute(value, axis, pairs)  9.72 us
  transfers between devices with their start and end apart: 15, of which 10 were waited for; matrix products, arithmetic and copies ran while one was open for 19% of the time, Pallas kernels for 0%

commit v1 on v0

v1 whole, which is shorter than its diff:
```python
import functools

import jax
import jax.numpy as jnp
import numpy as np
from jax import lax
from jax.experimental import pallas as pl
from jax.experimental.pallas import tpu as pltpu
from jax.sharding import PartitionSpec as P

SECTIONS = 4
TAPS = 4
EPS = 1e-6
MESH = pl.DeviceIdType.MESH
F32 = jnp.float32
BF16 = jnp.bfloat16


def angle_tables(beams):
    rows = []
    for s in range(SECTIONS):
        for h in range(2):
            for c in range(2):
                pos = np.float32(h * beams) + np.arange(beams, dtype=np.float32) + np.float32(0.5)
                rows.append(np.float32(2 * c - 1) * pos * np.float32(0.37 + 0.11 * s))
    psi = np.stack(rows).astype(np.float64)
    return np.cos(psi).astype(np.float32), np.sin(psi).astype(np.float32)


def kernel(
    n_rng,
    weights,
    taps,
    image,
    start,
    cosines,
    sines,
    merged,
    phase,
    own,
    got,
    matrix,
    acc0,
    acc1,
    acc2,
    prod,
    edge_out,
    edge_in,
    sums_out,
    sums_in,
    fac_out,
    fac_in,
    bulk_send,
    bulk_recv,
    edge_send,
    edge_recv,
    rim_send,
    rim_recv,
    sums_send,
    sums_recv,
    fac_send,
    fac_recv,
):
    sub = lax.axis_index("sub")
    rho = lax.axis_index("rng")
    beams = image.shape[1]
    rows = image.shape[2]
    total = rows + 16
    step = 128
    chunks = rows // step
    halves = [lax.rem(sub // 2**s, 2) for s in range(SECTIONS)]
    partners = [sub + 2**s * (1 - 2 * halves[s]) for s in range(SECTIONS)]
    peers = [lax.rem(rho + d, n_rng) for d in range(1, n_rng)]

    barrier = pltpu.get_barrier_semaphore()
    for s in range(SECTIONS):
        pl.semaphore_signal(barrier, inc=1, device_id=(partners[s], rho), device_id_type=MESH)
    for peer in peers:
        pl.semaphore_signal(barrier, inc=1, device_id=(sub, peer), device_id_type=MESH)

    def build(s):
        for which in range(2):
            half = halves[s]
            child = half if which == 0 else 1 - half
            row = s * 4 + half * 2 + child
            shift = lax.broadcasted_iota(jnp.int32, (beams, beams), 0) - start[pl.ds(row, 1), :]
            cos_row = cosines[pl.ds(row, 1), :]
            sin_row = sines[pl.ds(row, 1), :]
            real = jnp.zeros((beams, beams), F32)
            imag = jnp.zeros((beams, beams), F32)
            for t in range(TAPS):
                hit = shift == t
                real = jnp.where(hit, cos_row * weights[s * TAPS + t], real)
                imag = jnp.where(hit, sin_row * weights[s * TAPS + t], imag)
            matrix[s, which, 0:beams, 0:beams] = real.astype(BF16)
            matrix[s, which, 0:beams, beams : 2 * beams] = imag.astype(BF16)
            matrix[s, which, beams : 2 * beams, 0:beams] = (-imag).astype(BF16)
            matrix[s, which, beams : 2 * beams, beams : 2 * beams] = real.astype(BF16)

    for j in range(chunks):
        for part in range(2):
            block = image[part, :, j * step : (j + 1) * step].astype(F32)
            own[0, j * step : (j + 1) * step, part * beams : (part + 1) * beams] = block.T.astype(BF16)
    first = own[0, 0:16, :].astype(F32)
    last = own[0, rows - 16 : rows, :].astype(F32)
    edge_out[...] = jnp.concatenate([first[0:8], last[8:16]], axis=0).astype(BF16)

    pl.semaphore_wait(barrier, SECTIONS + n_rng - 1)

    def bulk(s):
        if s == 0:
            return pltpu.make_async_remote_copy(
                src_ref=own.at[0, pl.ds(0, rows)],
                dst_ref=got.at[0, pl.ds(0, rows)],
                send_sem=bulk_send.at[0],
                recv_sem=bulk_recv.at[0],
                device_id=(partners[0], rho),
                device_id_type=MESH,
            )
        return pltpu.make_async_remote_copy(
            src_ref=own.at[s],
            dst_ref=got.at[s],
            send_sem=bulk_send.at[s],
            recv_sem=bulk_recv.at[s],
            device_id=(partners[s], rho),
            device_id_type=MESH,
        )

    below, above = lax.rem(rho + n_rng - 1, n_rng), lax.rem(rho + 1, n_rng)

    def edge(side):
        return pltpu.make_async_remote_copy(
            src_ref=edge_out,
            dst_ref=edge_in.at[side],
            send_sem=edge_send.at[side],
            recv_sem=edge_recv.at[side],
            device_id=(sub, above if side == 0 else below),
            device_id_type=MESH,
        )

    rim = pltpu.make_async_remote_copy(
        src_ref=own.at[0, pl.ds(rows, 16)],
        dst_ref=got.at[0, pl.ds(rows, 16)],
        send_sem=rim_send.at[0],
        recv_sem=rim_recv.at[0],
        device_id=(partners[0], rho),
        device_id_type=MESH,
    )

    edge(0).start()
    edge(1).start()
    bulk(0).start()
    build(0)

    row_id = lax.broadcasted_iota(jnp.int32, (16, 2 * beams), 0)
    low = jnp.where(rho < n_rng - 1, 1.0, 0.0).astype(F32)
    high = jnp.where(rho > 0, 1.0, 0.0).astype(F32)
    mask = jnp.where(row_id < 8, low, high)

    edge(0).wait()
    edge(1).wait()
    halo = jnp.concatenate([edge_in[1].astype(F32)[0:8], edge_in[0].astype(F32)[8:16]], axis=0)
    own[0, rows:total, :] = (halo * mask).astype(BF16)
    rim.start()
    build(1)

    def rotated(ref, s, base, size, factor):
        value = ref[s, pl.ds(base, size), :]
        if factor is None:
            return value
        value = value.astype(F32)
        real, imag = value[:, :beams], value[:, beams:]
        g_re, g_im = factor
        return jnp.concatenate(
            [(real * g_re - imag * g_im).astype(BF16), (real * g_im + imag * g_re).astype(BF16)], axis=1
        )

    big = total // 3

    for s in range(SECTIONS):
        half = halves[s]
        if s == 0:
            own_factor = got_factor = None
        else:
            own_factor = (fac_out[s - 1, 0:1, :], fac_out[s - 1, 1:2, :])

        @pl.loop(0, 3)
        def _(i, s=s, factor=own_factor):
            base = pl.multiple_of(i * big, 16)
            prod[pl.ds(base, big), :] = jnp.dot(
                rotated(own, s, base, big, factor), matrix[s, 0], preferred_element_type=F32
            )

        if s == 0:
            rim.wait_recv()
        else:
            if s + 1 < SECTIONS:
                build(s + 1)
            factor_copy(s - 1).wait_recv()
            got_factor = (fac_in[s - 1, 0:1, :], fac_in[s - 1, 1:2, :])
        bulk(s).wait_recv()
        own_taps = [taps[s * 6 + half * 3 + k] for k in range(3)]
        got_taps = [taps[s * 6 + (1 - half) * 3 + k] for k in range(3)]

        @pl.loop(0, 3)
        def _(i, s=s, factor=got_factor, own_taps=own_taps, got_taps=got_taps):
            base = pl.multiple_of(i * big, 16)
            theirs = jnp.dot(rotated(got, s, base, big, factor), matrix[s, 1], preferred_element_type=F32)
            mine = prod[pl.ds(base, big), :]
            acc0[pl.ds(base + 8, big), :] = own_taps[0] * mine + got_taps[0] * theirs
            acc1[pl.ds(base, big), :] = own_taps[1] * mine + got_taps[1] * theirs
            acc2[pl.ds(base, big), :] = own_taps[2] * mine + got_taps[2] * theirs

        acc0[0:8, :] = acc0[total : total + 8, :]
        acc2[total : total + 8, :] = acc2[0:8, :]

        def merge(base, size):
            lower = acc0[pl.ds(base, size + 8), :][7 : 7 + size]
            upper = acc2[pl.ds(base, size + 8), :][1 : 1 + size]
            return acc1[pl.ds(base, size), :] + lower + upper

        sums = [jnp.zeros((8, beams), F32) for _ in range(3)]

        def tally(y, sums):
            real, imag = y[:, :beams], y[:, beams:]
            real_next, imag_next = pltpu.roll(real, beams - 1, 1), pltpu.roll(imag, beams - 1, 1)
            size = real.shape[0]
            terms = (
                real * real_next + imag * imag_next,
                real * imag_next - imag * real_next,
                (real * real + imag * imag) * (real_next * real_next + imag_next * imag_next),
            )
            return [
                a + jnp.sum(term.reshape(size // 8, 8, beams), axis=0) for a, term in zip(sums, terms)
            ]

        if s < SECTIONS - 1:
            piece = 64

            def body(i, sums, s=s):
                base = pl.multiple_of(i * piece, piece)
                y = merge(base, piece).astype(BF16)
                own[s + 1, pl.ds(base, piece), :] = y
                return tally(y.astype(F32), sums)

            sums = lax.fori_loop(0, rows // piece, body, sums)
            own[s + 1, rows:total, :] = (merge(rows, 16) * mask).astype(BF16)
        else:
            for j in range(chunks):
                y = merge(j * step, step).astype(BF16).astype(F32)
                for part in range(2):
                    merged[part, :, j * step : (j + 1) * step] = (
                        y[:, part * beams : (part + 1) * beams].T.astype(BF16)
                    )
                sums = tally(y, sums)

        line = lax.broadcasted_iota(jnp.int32, (8, beams), 0)
        packed = jnp.zeros((8, beams), F32)
        for k in range(3):
            packed = jnp.where(line == k, jnp.sum(sums[k], axis=0, keepdims=True), packed)
        sums_out[s] = packed
        sums_in[s, rho] = packed

        def sums_copy(d, s=s):
            return pltpu.make_async_remote_copy(
                src_ref=sums_out.at[s],
                dst_ref=sums_in.at[s, rho],
                send_sem=sums_send.at[s, d],
                recv_sem=sums_recv.at[s, d],
                device_id=(sub, peers[d]),
                device_id_type=MESH,
            )

        def sums_arrived(d, s=s):
            return pltpu.make_async_remote_copy(
                src_ref=sums_out.at[s],
                dst_ref=sums_in.at[s, peers[n_rng - 2 - d]],
                send_sem=sums_send.at[s, d],
                recv_sem=sums_recv.at[s, d],
                device_id=(sub, peers[d]),
                device_id_type=MESH,
            )

        for d in range(n_rng - 1):
            sums_copy(d).start()
        if s < SECTIONS - 1:
            bulk(s + 1).start()
        for d in range(n_rng - 1):
            sums_arrived(d).wait_recv()
        full = sums_in[s, 0]
        for other in range(1, n_rng):
            full = full + sums_in[s, other]
        scale = 1.0 / jnp.sqrt(full[2:3] + EPS)
        g_re, g_im = full[0:1] * scale, -(full[1:2] * scale)
        if s < SECTIONS - 1:
            fac_out[s] = jnp.where(line == 0, g_re, jnp.where(line == 1, g_im, 0.0))

            def factor_copy(s):
                return pltpu.make_async_remote_copy(
                    src_ref=fac_out.at[s],
                    dst_ref=fac_in.at[s],
                    send_sem=fac_send.at[s],
                    recv_sem=fac_recv.at[s],
                    device_id=(partners[s + 1], rho),
                    device_id_type=MESH,
                )

            factor_copy(s).start()
        else:
            phase[0:1, :] = g_re
            phase[1:2, :] = g_im

    rim.wait_send()
    for s in range(SECTIONS):
        bulk(s).wait_send()
        for d in range(n_rng - 1):
            pltpu.make_async_remote_copy(
                src_ref=sums_out.at[s],
                dst_ref=sums_in.at[s, rho],
                send_sem=sums_send.at[s, d],
                recv_sem=sums_recv.at[s, d],
                device_id=(sub, peers[d]),
                device_id_type=MESH,
            ).wait_send()
        if s < SECTIONS - 1:
            factor_copy(s).wait_send()


def solution(mesh):
    n_rng = mesh.shape["rng"]

    def on_device(image, stencil, interp_weights, range_taps):
        _, beams, rows = image.shape
        total = rows + 16
        cosines, sines = angle_tables(beams)
        start = stencil[..., 0].reshape(SECTIONS * 4, beams)
        vmem = pl.BlockSpec(memory_space=pltpu.VMEM)
        smem = pl.BlockSpec(memory_space=pltpu.SMEM)
        dma = pltpu.SemaphoreType.DMA
        return pl.pallas_call(
            functools.partial(kernel, n_rng),
            out_shape=(
                jax.ShapeDtypeStruct((2, beams, rows), BF16),
                jax.ShapeDtypeStruct((2, beams), F32),
            ),
            in_specs=[smem, smem, vmem, vmem, vmem, vmem],
            out_specs=(vmem, vmem),
            scratch_shapes=[
                pltpu.VMEM((SECTIONS, total, 2 * beams), BF16),
                pltpu.VMEM((SECTIONS, total, 2 * beams), BF16),
                pltpu.VMEM((SECTIONS, 2, 2 * beams, 2 * beams), BF16),
                pltpu.VMEM((total + 8, 2 * beams), F32),
                pltpu.VMEM((total, 2 * beams), F32),
                pltpu.VMEM((total + 8, 2 * beams), F32),
                pltpu.VMEM((total, 2 * beams), F32),
                pltpu.VMEM((16, 2 * beams), BF16),
                pltpu.VMEM((2, 16, 2 * beams), BF16),
                pltpu.VMEM((SECTIONS, 8, beams), F32),
                pltpu.VMEM((SECTIONS, n_rng, 8, beams), F32),
                pltpu.VMEM((SECTIONS - 1, 8, beams), F32),
                pltpu.VMEM((SECTIONS - 1, 8, beams), F32),
                dma((SECTIONS,)),
                dma((SECTIONS,)),
                dma((2,)),
                dma((2,)),
                dma((1,)),
                dma((1,)),
                dma((SECTIONS, n_rng - 1)),
                dma((SECTIONS, n_rng - 1)),
                dma((SECTIONS - 1,)),
                dma((SECTIONS - 1,)),
            ],
            compiler_params=pltpu.CompilerParams(
                collective_id=0, has_side_effects=True, vmem_limit_bytes=48 * 1024 * 1024
            ),
        )(
            interp_weights.reshape(-1),
            range_taps.reshape(-1),
            image,
            start,
            jnp.asarray(cosines),
            jnp.asarray(sines),
        )

    return jax.shard_map(
        on_device,
        mesh=mesh,
        in_specs=(P(None, "sub", "rng"), P(), P(), P()),
        out_specs=(P(None, "sub", "rng"), P(None, "sub")),
        check_vma=False,
    )
```

time: 229 us -> 97.8 us (0.43)
  Pallas kernels: 0 us -> 91.2 us
  blocking collectives: 86.4 us -> 0 us
  matrix products: 37.3 us -> 0 us
  starting transfers between devices: 32.5 us -> 0 us
  waiting for transfers between devices: 28.5 us -> 0 us
  other arithmetic: 25.8 us -> 0 us
  local copies, waits for them, and re-layouts: 15.5 us -> 5.64 us
    pallas_call x0 -> x1, Pallas kernels: none -> 91.2 us  [on_device(): pl.pallas_call(functools.partial(kernel, n_rng), out_shape=(jax.ShapeDtyp...]
    psum x8 -> x0, blocking collectives: 86.4 us -> none  [by_axis(): array = lax.psum(array, axis)]
    dot_general x48 -> x0, matrix products: 37.3 us -> none  [the longest x8 15.9 us: build_matrix(): matrix_im = jnp.einsum('at,atc->ac', coef_im, onehot).astype(jnp.bfloat16)]
    ppermute x15 -> x0, starting transfers between devices: 32.5 us -> none  [the longest x4 13.8 us: with_halo(): before = lax.ppermute(last, axis, up)]
    ppermute x15 -> x0, waiting for transfers between devices: 28.5 us -> none  [the longest x4 13.9 us: with_halo(): after = lax.ppermute(initial, axis, down)]
    add x5 -> x0, other arithmetic: 11.1 us -> none  [the longest x4 11 us: on_device(): lower_terms = taps_own[0] * own_terms + taps_partner[0] * partner_terms]
    convert_element_type x10 -> x0, other arithmetic: 10.1 us -> none  [the longest x6 6.89 us: rotate_rows(): values = blocks.astype(jnp.float32)]
    unnamed x54 -> x9, local copies, waits for them, and re-layouts: 9.01 us -> 3.89 us
  transfers between devices with their start and end apart: 15 -> 0, of which waited for: 10 -> 0; matrix products, arithmetic and copies ran while one was open for 19% -> 0% of each run, Pallas kernels for 0% -> 0%
where the time goes in v1:
time: 97.8 us; the launch traced here: 97.5 us
  Pallas kernels  91.2 us (93%)
  local copies, waits for them, and re-layouts  5.64 us (6%)
    pallas_call x1, Pallas kernels, on_device(): pl.pallas_call(functools.partial(kernel, n_rng), out_shape=(jax.ShapeDtyp...  91.2 us
    unnamed x9, local copies, waits for them, and re-layouts  3.89 us

profile of v1, /device:TPU:16, one launch (start us, length us, event | category | flops | bytes accessed | tf_op | source)
XLA Modules:
  0.0 97.5 jit_solution(1303928207119530466)
XLA Ops:
  0.6 0.8 reshape.10.weights
  1.4 0.8 copy.9
  2.2 0.1 reshape.11.taps
  2.3 0.9 slice_reduce_fusion
  3.1 0.0 copy-start.1
  3.2 0.0 copy-start.2
  3.2 0.7 copy-done.1
  3.9 0.0 copy-done.2
  3.9 0.0 copy-start
  3.9 1.0 %copy-done = bf16[2,256,512]{2,1,0:T(8,128)(2,1)S(1)} copy-done((bf16[2,256,512]{2,1,0:T(8,128)(2,1)S(1)}, bf16[2,256,512]{2,1,0:T(8,128)(2,1)}, u32[]{:S(2)}) %copy-start) | copy-done | bytes 524312
  4.9 91.2 %shard_map.77 = (bf16[2,256,512]{2,1,0:T(8,128)(2,1)S(1)}, f32[2,256]{1,0:T(2,128)S(1)}) custom-call(f32[16]{0:T(128)S(1)} %reshape.10.weights, f32[24]{0:T(128)S(1)} %reshape.11.taps, bf16[2,256,512]{2,1,0:T(8,128)(2,1)S(1)} %copy-done, s32[16,256]{1,0:T(8,128)S(1)} %reshape_squeeze.3.start, f32[16,256]{1,0:T(8,128)S(1)} %copy-done.2, f32[16,256]{1,0:T(8,128)S(1)} %copy-done.1), custom_call_target="tpu_custom_call" | custom-call | tf_op jit(solution)/shard_map/pallas_call | solution.py:340
  96.1 0.8 copy.13
  96.9 0.6 copy.14
  (1 shorter events, 0.0 us)
Async XLA Ops:
  3.1 0.7 copy-start.1
  3.2 0.7 copy-start.2
  3.9 1.0 %copy-start = (bf16[2,256,512]{2,1,0:T(8,128)(2,1)S(1)}, bf16[2,256,512]{2,1,0:T(8,128)(2,1)}, u32[]{:S(2)}) copy-start(bf16[2,256,512]{2,1,0:T(8,128)(2,1)} %image.1) | copy-start | bytes 1572868

commit v2 on v1

v2 whole, which is shorter than its diff:
```python
import functools

import jax
import jax.numpy as jnp
import numpy as np
from jax import lax
from jax.experimental import pallas as pl
from jax.experimental.pallas import tpu as pltpu
from jax.sharding import PartitionSpec as P

SECTIONS = 4
TAPS = 4
EPS = 1e-6
STEP = 128
EARLY = [lambda k: 0, lambda k: 0, lambda k: k - 3, lambda k: 0]
MIDDLE = [lambda k: 3, lambda k: 2, lambda k: k, lambda k: 0]
MESH = pl.DeviceIdType.MESH
F32 = jnp.float32
BF16 = jnp.bfloat16


def angle_tables(beams):
    rows = []
    for s in range(SECTIONS):
        for h in range(2):
            for c in range(2):
                pos = np.float32(h * beams) + np.arange(beams, dtype=np.float32) + np.float32(0.5)
                rows.append(np.float32(2 * c - 1) * pos * np.float32(0.37 + 0.11 * s))
    psi = np.stack(rows).astype(np.float64)
    return np.cos(psi).astype(np.float32), np.sin(psi).astype(np.float32)


def plan(order, n):
    done, out = set(), []
    groups = []
    for piece in order:
        done.add(piece)
        ready = [
            p
            for p in [n] + list(range(n))
            if p not in out and {p, (p + 1) % (n + 1), (p - 1) % (n + 1)} <= done
        ]
        out += ready
        groups.append(ready)
    return groups, out


def kernel(
    n_rng,
    weights,
    taps,
    image_hbm,
    stencil_hbm,
    trig_hbm,
    merged,
    phase,
    image,
    stencil,
    trig,
    own,
    got,
    matrix,
    acc0,
    acc1,
    acc2,
    prod,
    edge_out,
    edge_in,
    sums_out,
    sums_in,
    sums_far,
    fac_out,
    fac_in,
    load_sem,
    bulk_send,
    bulk_recv,
    edge_send,
    edge_recv,
    sums_send,
    sums_recv,
    far_send,
    far_recv,
    fac_send,
    fac_recv,
):
    sub = lax.axis_index("sub")
    rho = lax.axis_index("rng")
    beams = image.shape[1]
    rows = image.shape[2]
    total = rows + 16
    n = rows // STEP
    last = SECTIONS - 1
    halves = [lax.rem(sub // 2**s, 2) for s in range(SECTIONS)]
    partners = [sub + 2**s * (1 - 2 * halves[s]) for s in range(SECTIONS)]
    peers = [lax.rem(rho + d, n_rng) for d in range(1, n_rng)]

    barrier = pltpu.get_barrier_semaphore()
    for s in range(SECTIONS):
        pl.semaphore_signal(barrier, inc=1, device_id=(partners[s], rho), device_id_type=MESH)
    for peer in peers:
        pl.semaphore_signal(barrier, inc=1, device_id=(sub, peer), device_id_type=MESH)
        pl.semaphore_signal(barrier, inc=1, device_id=(partners[last], peer), device_id_type=MESH)

    loads = [
        pltpu.make_async_copy(image_hbm, image, load_sem.at[0]),
        pltpu.make_async_copy(stencil_hbm, stencil, load_sem.at[1]),
        pltpu.make_async_copy(trig_hbm, trig, load_sem.at[2]),
    ]
    for load in loads:
        load.start()

    def build(s):
        for which in range(2):
            half = halves[s]
            child = half if which == 0 else 1 - half
            row = s * 4 + half * 2 + child
            shift = lax.broadcasted_iota(jnp.int32, (beams, beams), 0) - stencil[row, 0:1, :]
            cos_row = trig[0, pl.ds(row, 1), :]
            sin_row = trig[1, pl.ds(row, 1), :]
            real = jnp.zeros((beams, beams), F32)
            imag = jnp.zeros((beams, beams), F32)
            for t in range(TAPS):
                hit = shift == t
                real = jnp.where(hit, cos_row * weights[s, t], real)
                imag = jnp.where(hit, sin_row * weights[s, t], imag)
            matrix[s, which, 0:beams, 0:beams] = real.astype(BF16)
            matrix[s, which, 0:beams, beams : 2 * beams] = imag.astype(BF16)
            matrix[s, which, beams : 2 * beams, 0:beams] = (-imag).astype(BF16)
            matrix[s, which, beams : 2 * beams, beams : 2 * beams] = real.astype(BF16)

    for load in loads:
        load.wait()
    for j in range(rows // 128):
        for part in range(2):
            block = image[part, :, j * 128 : (j + 1) * 128].astype(F32)
            own[0, j * 128 : (j + 1) * 128, part * beams : (part + 1) * beams] = block.T.astype(BF16)
    low_edge = own[0, 0:16, :].astype(F32)
    high_edge = own[0, rows - 16 : rows, :].astype(F32)
    edge_out[...] = jnp.concatenate([low_edge[0:8], high_edge[8:16]], axis=0).astype(BF16)

    pl.semaphore_wait(barrier, SECTIONS + 2 * (n_rng - 1))

    def span(piece):
        return (rows, 16) if piece == n else (piece * STEP, STEP)

    def bulk(s, piece):
        base, size = (0, rows) if s == 0 and piece == 0 else span(piece)
        return pltpu.make_async_remote_copy(
            src_ref=own.at[s, pl.ds(base, size)],
            dst_ref=got.at[s, pl.ds(base, size)],
            send_sem=bulk_send.at[s, piece],
            recv_sem=bulk_recv.at[s, piece],
            device_id=(partners[s], rho),
            device_id_type=MESH,
        )

    below, above = lax.rem(rho + n_rng - 1, n_rng), lax.rem(rho + 1, n_rng)

    def edge(side):
        return pltpu.make_async_remote_copy(
            src_ref=edge_out,
            dst_ref=edge_in.at[side],
            send_sem=edge_send.at[side],
            recv_sem=edge_recv.at[side],
            device_id=(sub, above if side == 0 else below),
            device_id_type=MESH,
        )

    edge(0).start()
    edge(1).start()
    bulk(0, 0).start()
    build(0)

    row_id = lax.broadcasted_iota(jnp.int32, (16, 2 * beams), 0)
    low = jnp.where(rho < n_rng - 1, 1.0, 0.0).astype(F32)
    high = jnp.where(rho > 0, 1.0, 0.0).astype(F32)
    mask = jnp.where(row_id < 8, low, high)

    edge(0).wait()
    edge(1).wait()
    halo = jnp.concatenate([edge_in[1].astype(F32)[0:8], edge_in[0].astype(F32)[8:16]], axis=0)
    own[0, rows:total, :] = (halo * mask).astype(BF16)
    bulk(0, n).start()

    def rotated(ref, s, base, size, factor):
        value = ref[s, pl.ds(base, size), :]
        if factor is None:
            return value
        value = value.astype(F32)
        real, imag = value[:, :beams], value[:, beams:]
        g_re, g_im = factor
        return jnp.concatenate(
            [(real * g_re - imag * g_im).astype(BF16), (real * g_im + imag * g_re).astype(BF16)], axis=1
        )

    def gathered(ref, slot):
        full = ref[slot, 0]
        for other in range(1, n_rng):
            full = full + ref[slot, other]
        scale = 1.0 / jnp.sqrt(full[2:3] + EPS)
        return full[0:1] * scale, -(full[1:2] * scale)

    def merge(base, size):
        lower = acc0[base : base + size + 8, :][7 : 7 + size]
        upper = acc2[base : base + size + 8, :][1 : 1 + size]
        return acc1[base : base + size, :] + lower + upper

    def tally(y, sums):
        real, imag = y[:, :beams], y[:, beams:]
        real_next, imag_next = pltpu.roll(real, beams - 1, 1), pltpu.roll(imag, beams - 1, 1)
        size = real.shape[0]
        terms = (
            real * real_next + imag * imag_next,
            real * imag_next - imag * real_next,
            (real * real + imag * imag) * (real_next * real_next + imag_next * imag_next),
        )
        return [a + jnp.sum(term.reshape(size // 8, 8, beams), axis=0) for a, term in zip(sums, terms)]

    def sums_copy(s, d, slot):
        return pltpu.make_async_remote_copy(
            src_ref=sums_out.at[s],
            dst_ref=sums_in.at[s, slot],
            send_sem=sums_send.at[s, d],
            recv_sem=sums_recv.at[s, d],
            device_id=(sub, peers[d]),
            device_id_type=MESH,
        )

    def far_copy(d, slot):
        return pltpu.make_async_remote_copy(
            src_ref=sums_out.at[last - 1],
            dst_ref=sums_far.at[0, slot],
            send_sem=far_send.at[d],
            recv_sem=far_recv.at[d],
            device_id=(partners[last], rho if d == n_rng - 1 else peers[d]),
            device_id_type=MESH,
        )

    def factor_copy(s):
        return pltpu.make_async_remote_copy(
            src_ref=fac_out.at[s],
            dst_ref=fac_in.at[s],
            send_sem=fac_send.at[s],
            recv_sem=fac_recv.at[s],
            device_id=(partners[s + 1], rho),
            device_id_type=MESH,
        )

    line = lax.broadcasted_iota(jnp.int32, (8, beams), 0)
    big = total // 3
    order = [0, n]
    own_factor = got_factor = None

    for s in range(SECTIONS):
        half = halves[s]

        @pl.loop(0, 3)
        def _(i, s=s, factor=own_factor):
            base = pl.multiple_of(i * big, 16)
            prod[pl.ds(base, big), :] = jnp.dot(
                rotated(own, s, base, big, factor), matrix[s, 0], preferred_element_type=F32
            )

        if s < last:
            build(s + 1)
        if 0 < s < last:
            factor_copy(s - 1).wait_recv()
            got_factor = (fac_in[s - 1, 0:1, :], fac_in[s - 1, 1:2, :])
        own_taps = [taps[k, half, s] for k in range(3)]
        got_taps = [taps[k, 1 - half, s] for k in range(3)]

        def combine(base, size, s=s, factor=got_factor, own_taps=own_taps, got_taps=got_taps):
            theirs = jnp.dot(rotated(got, s, base, size, factor), matrix[s, 1], preferred_element_type=F32)
            mine = prod[pl.ds(base, size), :]
            acc0[pl.ds(base + 8, size), :] = own_taps[0] * mine + got_taps[0] * theirs
            acc1[pl.ds(base, size), :] = own_taps[1] * mine + got_taps[1] * theirs
            acc2[pl.ds(base, size), :] = own_taps[2] * mine + got_taps[2] * theirs

        sums = [jnp.zeros((8, beams), F32) for _ in range(3)]
        if s == 0:
            bulk(0, 0).wait_recv()
            bulk(0, n).wait_recv()

            @pl.loop(0, 3)
            def _(i):
                combine(pl.multiple_of(i * big, 16), big)

            acc0[0:8, :] = acc0[total : total + 8, :]
            acc2[total : total + 8, :] = acc2[0:8, :]
            groups, produced = [[n] + list(range(n))], [n] + list(range(n))
        else:
            groups, produced = plan(order, n)
        if s == last:
            bulk(0, 0).wait_send()
            bulk(0, n).wait_send()
        early, middle = EARLY[s](len(produced)), MIDDLE[s](len(produced))
        sent = 0
        for g, group in enumerate(groups):
            if s > 0:
                piece = order[g]
                bulk(s, piece).wait_recv()
                base, size = span(piece)
                combine(base, size)
                if piece == n:
                    acc0[0:8, :] = acc0[total : total + 8, :]
                if piece == 0:
                    acc2[total : total + 8, :] = acc2[0:8, :]
            for piece in group:
                base, size = span(piece)
                if s == last:
                    if piece == n:
                        continue
                    y = merge(base, size).astype(BF16)
                    own[0, base : base + size, :] = y
                    sums = tally(y.astype(F32), sums)
                    continue
                if piece == n:
                    own[s + 1, rows:total, :] = (merge(rows, 16) * mask).astype(BF16)
                else:
                    y = merge(base, size).astype(BF16)
                    own[s + 1, base : base + size, :] = y
                    sums = tally(y.astype(F32), sums)
                if sent < early:
                    bulk(s + 1, piece).start()
                    sent += 1

        packed = jnp.zeros((8, beams), F32)
        for k in range(3):
            packed = jnp.where(line == k, jnp.sum(sums[k], axis=0, keepdims=True), packed)
        sums_out[s] = packed
        sums_in[s, rho] = packed
        for d in range(n_rng - 1):
            sums_copy(s, d, rho).start()
        if s == last - 1:
            for d in range(n_rng):
                far_copy(d, rho).start()
        if s < last:
            while sent < middle:
                bulk(s + 1, produced[sent]).start()
                sent += 1
        else:
            for j in range(rows // 128):
                y = own[0, j * 128 : (j + 1) * 128, :].astype(F32)
                for part in range(2):
                    merged[part, :, j * 128 : (j + 1) * 128] = (
                        y[:, part * beams : (part + 1) * beams].T.astype(BF16)
                    )
        for d in range(n_rng - 1):
            sums_copy(s, d, peers[n_rng - 2 - d]).wait_recv()
        g_re, g_im = gathered(sums_in, s)
        if s < last:
            own_factor = (g_re, g_im)
            if s < last - 1:
                fac_out[s] = jnp.where(line == 0, g_re, jnp.where(line == 1, g_im, 0.0))
                factor_copy(s).start()
            while sent < len(produced):
                bulk(s + 1, produced[sent]).start()
                sent += 1
            if s == last - 1:
                for d in range(n_rng - 1):
                    far_copy(d, peers[n_rng - 2 - d]).wait_recv()
                far_copy(n_rng - 1, rho).wait_recv()
                got_factor = gathered(sums_far, 0)
        else:
            phase[0:1, :] = g_re
            phase[1:2, :] = g_im
        order = produced

    for s in range(SECTIONS):
        if s > 0:
            for piece in range(n + 1):
                bulk(s, piece).wait_send()
        for d in range(n_rng - 1):
            sums_copy(s, d, rho).wait_send()
        if s < last - 1:
            factor_copy(s).wait_send()
    for d in range(n_rng):
        far_copy(d, rho).wait_send()


def solution(mesh):
    n_rng = mesh.shape["rng"]

    def on_device(image, stencil, interp_weights, range_taps):
        _, beams, rows = image.shape
        total = rows + 16
        cosines, sines = angle_tables(beams)
        pieces = rows // STEP + 1
        hbm = pl.BlockSpec(memory_space=pltpu.HBM)
        vmem = pl.BlockSpec(memory_space=pltpu.VMEM)
        smem = pl.BlockSpec(memory_space=pltpu.SMEM)
        dma = pltpu.SemaphoreType.DMA
        return pl.pallas_call(
            functools.partial(kernel, n_rng),
            out_shape=(
                jax.ShapeDtypeStruct((2, beams, rows), BF16),
                jax.ShapeDtypeStruct((2, beams), F32),
            ),
            in_specs=[smem, smem, hbm, hbm, hbm],
            out_specs=(vmem, vmem),
            scratch_shapes=[
                pltpu.VMEM((2, beams, rows), BF16),
                pltpu.VMEM((SECTIONS * 4, TAPS, beams), jnp.int32),
                pltpu.VMEM((2, SECTIONS * 4, beams), F32),
                pltpu.VMEM((SECTIONS, total, 2 * beams), BF16),
                pltpu.VMEM((SECTIONS, total, 2 * beams), BF16),
                pltpu.VMEM((SECTIONS, 2, 2 * beams, 2 * beams), BF16),
                pltpu.VMEM((total + 8, 2 * beams), F32),
                pltpu.VMEM((total, 2 * beams), F32),
                pltpu.VMEM((total + 8, 2 * beams), F32),
                pltpu.VMEM((total, 2 * beams), F32),
                pltpu.VMEM((16, 2 * beams), BF16),
                pltpu.VMEM((2, 16, 2 * beams), BF16),
                pltpu.VMEM((SECTIONS, 8, beams), F32),
                pltpu.VMEM((SECTIONS, n_rng, 8, beams), F32),
                pltpu.VMEM((1, n_rng, 8, beams), F32),
                pltpu.VMEM((SECTIONS - 2, 8, beams), F32),
                pltpu.VMEM((SECTIONS - 2, 8, beams), F32),
                dma((3,)),
                dma((SECTIONS, pieces)),
                dma((SECTIONS, pieces)),
                dma((2,)),
                dma((2,)),
                dma((SECTIONS, n_rng - 1)),
                dma((SECTIONS, n_rng - 1)),
                dma((n_rng,)),
                dma((n_rng,)),
                dma((SECTIONS - 2,)),
                dma((SECTIONS - 2,)),
            ],
            compiler_params=pltpu.CompilerParams(
                collective_id=0, has_side_effects=True, vmem_limit_bytes=67043328
            ),
        )(
            interp_weights,
            range_taps.transpose(2, 1, 0),
            image,
            stencil.transpose(0, 1, 2, 4, 3).reshape(SECTIONS * 4, TAPS, beams),
            jnp.asarray(np.stack([cosines, sines])),
        )

    return jax.shard_map(
        on_device,
        mesh=mesh,
        in_specs=(P(None, "sub", "rng"), P(), P(), P()),
        out_specs=(P(None, "sub", "rng"), P(None, "sub")),
        check_vma=False,
    )
```

time: 97.8 us -> 88.7 us (0.907)
  Pallas kernels: 91.2 us -> 84.9 us
  local copies, waits for them, and re-layouts: 5.64 us -> 2.45 us
    pallas_call x1, Pallas kernels: 91.2 us -> 84.9 us  [on_device(): pl.pallas_call(functools.partial(kernel, n_rng), out_shape=(jax.ShapeDtyp...]
    unnamed x9 -> x4, local copies, waits for them, and re-layouts: 3.89 us -> 2.45 us
where the time goes in v2:
time: 88.7 us; the launch traced here: 88 us
  Pallas kernels  84.9 us (96%)
  local copies, waits for them, and re-layouts  2.45 us (3%)
    pallas_call x1, Pallas kernels, on_device(): pl.pallas_call(functools.partial(kernel, n_rng), out_shape=(jax.ShapeDtyp...  84.9 us
    unnamed x4, local copies, waits for them, and re-layouts  2.45 us

profile of v2, /device:TPU:16, one launch (start us, length us, event | category | flops | bytes accessed | tf_op | source)
XLA Modules:
  0.0 88.0 jit_solution(6809554585249701850)
XLA Ops:
  0.6 84.9 %shard_map.68 = (bf16[2,256,512]{2,1,0:T(8,128)(2,1)}, f32[2,256]{1,0:T(2,128)}) custom-call(f32[4,4]{1,0:T(4,128)} %weights.1, f32[3,2,4]{2,1,0:T(2,128)} %bitcast.5, bf16[2,256,512]{2,1,0:T(8,128)(2,1)} %image_hbm.1, s32[16,4,256]{2,1,0:T(4,128)} %bitcast.4, f32[2,16,256]{2,1,0:T(8,128)} %constant.2.clone.trig_hbm), custom_call_target="tpu_custom_call" | custom-call | tf_op jit(solution)/shard_map/pallas_call | solution.py:393
  85.6 0.0 copy-start
  85.6 1.9 %copy.9 = bf16[2,256,512]{2,1,0:T(8,128)(2,1)} copy(bf16[2,256,512]{2,1,0:T(8,128)(2,1)} %get-tuple-element.4) | data formatting | bytes 1048576
  87.5 0.0 copy-done
  87.5 0.6 copy.10
Async XLA Ops:
  85.6 1.9 %copy-start = (f32[2,256]{1,0:T(2,128)S(1)}, f32[2,256]{1,0:T(2,128)}, u32[]{:S(2)}) copy-start(f32[2,256]{1,0:T(2,128)} %get-tuple-element.5) | copy-start | bytes 6148

commit v3 on v2

v3 whole, which is shorter than its diff:
```python
import functools

import jax
import jax.numpy as jnp
import numpy as np
from jax import lax
from jax.experimental import pallas as pl
from jax.experimental.pallas import tpu as pltpu
from jax.sharding import PartitionSpec as P

SECTIONS = 4
TAPS = 4
EPS = 1e-6
QUARTERS = 4
CHUNK = 128
WITH_RIM = CHUNK + 16
MESH = pl.DeviceIdType.MESH
F32 = jnp.float32
BF16 = jnp.bfloat16


def angle_tables(beams):
    rows = []
    for s in range(SECTIONS):
        for h in range(2):
            for c in range(2):
                pos = np.float32(h * beams) + np.arange(beams, dtype=np.float32) + np.float32(0.5)
                rows.append(np.float32(2 * c - 1) * pos * np.float32(0.37 + 0.11 * s))
    psi = np.stack(rows).astype(np.float64)
    return np.cos(psi).astype(np.float32), np.sin(psi).astype(np.float32)


def kernel(
    n_rng,
    weights,
    taps,
    image_hbm,
    stencil_hbm,
    trig_hbm,
    merged,
    phase,
    image,
    stencil,
    trig,
    own,
    got,
    matrix,
    acc0,
    acc1,
    acc2,
    prod,
    edge_out,
    edge_in,
    sums_out,
    sums_in,
    split_out,
    split_in,
    stacked,
    terms,
    middle_y,
    back_out,
    back_in,
    far_in,
    fac_out,
    fac_in,
    far_fac_out,
    far_fac_in,
    wide_out,
    wide_in,
    part_out,
    part_in,
    load_sem,
    core_send,
    core_recv,
    edge_send,
    edge_recv,
    sums_send,
    sums_recv,
    split_send,
    split_recv,
    back_send,
    back_recv,
    far_send,
    far_recv,
    fac_send,
    fac_recv,
    wide_send,
    wide_recv,
    part_send,
    part_recv,
):
    sub = lax.axis_index("sub")
    rho = lax.axis_index("rng")
    beams = image.shape[1]
    rows = image.shape[2]
    total = rows + 16
    width = 2 * beams
    quarter = lax.rem(sub // 2, QUARTERS)
    core_half = lax.rem(sub, 2)
    y_half = lax.rem(sub // 8, 2)
    core_partner = sub + 1 - 2 * core_half
    y_partner = sub + 8 * (1 - 2 * y_half)
    ahead = [lax.rem(quarter + e, QUARTERS) for e in range(QUARTERS)]
    behind = [lax.rem(quarter + QUARTERS - e, QUARTERS) for e in range(QUARTERS)]
    peers = [lax.rem(rho + d, n_rng) for d in range(1, n_rng)]

    def at_quarter(other):
        return sub + 2 * (other - quarter)

    barrier = pltpu.get_barrier_semaphore()
    for other in (core_partner, y_partner, *[at_quarter(ahead[e]) for e in range(1, QUARTERS)]):
        pl.semaphore_signal(barrier, inc=1, device_id=(other, rho), device_id_type=MESH)
    for peer in peers:
        pl.semaphore_signal(barrier, inc=1, device_id=(sub, peer), device_id_type=MESH)

    loads = [
        pltpu.make_async_copy(image_hbm, image, load_sem.at[0]),
        pltpu.make_async_copy(stencil_hbm, stencil, load_sem.at[1]),
        pltpu.make_async_copy(trig_hbm, trig, load_sem.at[2]),
    ]
    for load in loads:
        load.start()

    def build(slot, s, half, child):
        row = s * 4 + half * 2 + child
        shift = lax.broadcasted_iota(jnp.int32, (beams, beams), 0) - stencil[row, 0:1, :]
        cos_row = trig[0, pl.ds(row, 1), :]
        sin_row = trig[1, pl.ds(row, 1), :]
        real = jnp.zeros((beams, beams), F32)
        imag = jnp.zeros((beams, beams), F32)
        for t in range(TAPS):
            hit = shift == t
            real = jnp.where(hit, cos_row * weights[s, t], real)
            imag = jnp.where(hit, sin_row * weights[s, t], imag)
        matrix[slot, 0:beams, 0:beams] = real.astype(BF16)
        matrix[slot, 0:beams, beams:width] = imag.astype(BF16)
        matrix[slot, beams:width, 0:beams] = (-imag).astype(BF16)
        matrix[slot, beams:width, beams:width] = real.astype(BF16)

    def copy_to(src, dst, send, recv, target):
        return pltpu.make_async_remote_copy(
            src_ref=src, dst_ref=dst, send_sem=send, recv_sem=recv, device_id=target, device_id_type=MESH
        )

    for load in loads:
        load.wait()
    for j in range(rows // CHUNK):
        for part in range(2):
            block = image[part, :, j * CHUNK : (j + 1) * CHUNK].astype(F32)
            own[j * CHUNK : (j + 1) * CHUNK, part * beams : (part + 1) * beams] = block.T.astype(BF16)
    low_edge = own[0:16, :].astype(F32)
    high_edge = own[rows - 16 : rows, :].astype(F32)
    edge_out[...] = jnp.concatenate([low_edge[0:8], high_edge[8:16]], axis=0).astype(BF16)
    build(0, 0, core_half, core_half)
    build(1, 0, core_half, 1 - core_half)

    pl.semaphore_wait(barrier, 1 + 1 + QUARTERS - 1 + n_rng - 1)

    def core_copy(rim):
        base, size = (rows, 16) if rim else (0, rows)
        return copy_to(
            own.at[pl.ds(base, size)], got.at[pl.ds(base, size)], core_send.at[rim], core_recv.at[rim], (core_partner, rho)
        )

    below, above = lax.rem(rho + n_rng - 1, n_rng), lax.rem(rho + 1, n_rng)

    def edge(side):
        return copy_to(
            edge_out, edge_in.at[side], edge_send.at[side], edge_recv.at[side], (sub, above if side == 0 else below)
        )

    edge(0).start()
    edge(1).start()
    core_copy(0).start()

    row_id = lax.broadcasted_iota(jnp.int32, (16, width), 0)
    one = jnp.float32(1.0)
    spot = rho * QUARTERS + quarter
    low = jnp.where(rho < n_rng - 1, one, 0.0)
    high = jnp.where(rho > 0, one, 0.0)
    mask = jnp.where(row_id < 8, low, high)
    low = jnp.where(spot < n_rng * QUARTERS - 1, one, 0.0)
    high = jnp.where(spot > 0, one, 0.0)
    chunk_mask = jnp.where(row_id < 8, low, high)

    def rotate(value, g_re, g_im):
        value = value.astype(F32)
        real, imag = value[:, :beams], value[:, beams:]
        return jnp.concatenate(
            [(real * g_re - imag * g_im).astype(BF16), (real * g_im + imag * g_re).astype(BF16)], axis=1
        )

    def factors(re, im, power):
        scale = 1.0 / jnp.sqrt(power + EPS)
        return re * scale, -(im * scale)

    def tally(y, sums):
        real, imag = y[:, :beams], y[:, beams:]
        real_next, imag_next = pltpu.roll(real, beams - 1, 1), pltpu.roll(imag, beams - 1, 1)
        size = real.shape[0]
        products = (
            real * real_next + imag * imag_next,
            real * imag_next - imag * real_next,
            (real * real + imag * imag) * (real_next * real_next + imag_next * imag_next),
        )
        return [a + jnp.sum(p.reshape(size // 8, 8, beams), axis=0) for a, p in zip(sums, products)]

    def zeros():
        return [jnp.zeros((8, beams), F32) for _ in range(3)]

    def spread(base, size, mine, theirs, taps_mine, taps_theirs):
        acc0[pl.ds(base + 8, size), :] = taps_mine[0] * mine + taps_theirs[0] * theirs
        acc1[pl.ds(base, size), :] = taps_mine[1] * mine + taps_theirs[1] * theirs
        acc2[pl.ds(base, size), :] = taps_mine[2] * mine + taps_theirs[2] * theirs

    def close(length):
        acc0[0:8, :] = acc0[length : length + 8, :]
        acc2[length : length + 8, :] = acc2[0:8, :]

    def merge(base, size):
        lower = acc0[base : base + size + 8, :][7 : 7 + size]
        upper = acc2[base : base + size + 8, :][1 : 1 + size]
        return (acc1[base : base + size, :] + lower + upper).astype(BF16)

    line = lax.broadcasted_iota(jnp.int32, (8, beams), 0)

    def sums_copy(s, d, slot):
        return copy_to(
            sums_out.at[s], sums_in.at[s, slot], sums_send.at[s, d], sums_recv.at[s, d], (sub, peers[d])
        )

    def send_sums(s, sums):
        packed = jnp.zeros((8, beams), F32)
        for k in range(3):
            packed = jnp.where(line == k, jnp.sum(sums[k], axis=0, keepdims=True), packed)
        sums_out[s] = packed
        sums_in[s, rho] = packed
        for d in range(n_rng - 1):
            sums_copy(s, d, rho).start()

    def take_sums(s):
        for d in range(n_rng - 1):
            sums_copy(s, d, peers[n_rng - 2 - d]).wait_recv()
        full = sums_in[s, 0]
        for other in range(1, n_rng):
            full = full + sums_in[s, other]
        return factors(full[0:1], full[1:2], full[2:3])

    half_rows = rows // 2

    @pl.loop(0, 2)
    def _(i):
        base = pl.multiple_of(i * half_rows, 16)
        prod[pl.ds(base, half_rows), :] = jnp.dot(
            own[pl.ds(base, half_rows), :], matrix[0], preferred_element_type=F32
        )

    core_mine = [taps[k, core_half, 0] for k in range(3)]
    core_theirs = [taps[k, 1 - core_half, 0] for k in range(3)]
    core_copy(0).wait_recv()

    @pl.loop(0, 2)
    def _(i):
        base = pl.multiple_of(i * half_rows, 16)
        theirs = jnp.dot(got[pl.ds(base, half_rows), :], matrix[1], preferred_element_type=F32)
        spread(base, half_rows, prod[pl.ds(base, half_rows), :], theirs, core_mine, core_theirs)

    edge(0).wait()
    edge(1).wait()
    halo = jnp.concatenate([edge_in[1].astype(F32)[0:8], edge_in[0].astype(F32)[8:16]], axis=0)
    own[rows:total, :] = (halo * mask).astype(BF16)
    core_copy(1).start()
    mine = jnp.dot(own[rows:total, :], matrix[0], preferred_element_type=F32)
    core_copy(1).wait_recv()
    theirs = jnp.dot(got[rows:total, :], matrix[1], preferred_element_type=F32)
    spread(rows, 16, mine, theirs, core_mine, core_theirs)
    close(total)
    sums = zeros()
    for j in range(QUARTERS):
        y = merge(j * CHUNK, CHUNK)
        split_out[j, 0:CHUNK, :] = y
        y = y.astype(F32)
        sums = tally(y, sums)
        prod[j * CHUNK : j * CHUNK + 8, :] = y[0:8]
        prod[(j + 1) * CHUNK - 8 : (j + 1) * CHUNK, :] = y[CHUNK - 8 : CHUNK]
    send_sums(0, sums)
    prod[rows:total, :] = merge(rows, 16).astype(F32) * mask
    for j in range(QUARTERS):
        after = (j + 1) * CHUNK
        before = (j * CHUNK - 8) % total
        split_out[j, CHUNK:WITH_RIM, :] = jnp.concatenate(
            [prod[after : after + 8, :], prod[before : before + 8, :]], axis=0
        ).astype(BF16)

    def split(e, slot):
        return copy_to(
            split_out.at[ahead[e]],
            split_in.at[slot],
            split_send.at[e - 1],
            split_recv.at[e - 1],
            (at_quarter(ahead[e]), rho),
        )

    def fac(e, slot):
        return copy_to(
            fac_out, fac_in.at[slot], fac_send.at[e - 1], fac_recv.at[e - 1], (at_quarter(ahead[e]), rho)
        )

    split(2, quarter).start()
    split_in[quarter] = split_out[quarter]
    g_re, g_im = take_sums(0)
    packed = jnp.where(line == 0, g_re, jnp.where(line == 1, g_im, 0.0))
    fac_out[...] = packed
    fac_in[quarter] = packed
    for e in (1, 3, 2):
        fac(e, quarter).start()
    split(1, quarter).start()
    split(3, quarter).start()

    for half in range(2):
        for child in range(2):
            build(2 + half * 2 + child, 1, half, child)
            build(6 + half * 2 + child, 2, half, child)
    build(10, 3, y_half, y_half)
    build(11, 3, y_half, 1 - y_half)

    def wide_copy(t, d, slot):
        return copy_to(
            wide_out.at[t], wide_in.at[t, slot], wide_send.at[t, d], wide_recv.at[t, d], (sub, peers[d])
        )

    def part_copy(t, e, slot):
        return copy_to(
            part_out.at[t],
            part_in.at[t, slot],
            part_send.at[t, e - 1],
            part_recv.at[t, e - 1],
            (at_quarter(ahead[e]), rho),
        )

    tall = lax.broadcasted_iota(jnp.int32, (16, beams), 0)

    def cross(t, target):
        s = t + 1
        packed = jnp.zeros((16, beams), F32)
        for half in range(2):
            for child in range(2):
                terms[child] = jnp.dot(
                    stacked[child], matrix[2 + 4 * t + half * 2 + child], preferred_element_type=F32
                )
            for pair in range(2):
                block = 2 * pair + half if t == 0 else 2 * half + pair
                at = pair * WITH_RIM
                spread(
                    0,
                    WITH_RIM,
                    terms[0, at : at + WITH_RIM, :],
                    terms[1, at : at + WITH_RIM, :],
                    [taps[k, 0, s] for k in range(3)],
                    [taps[k, 1, s] for k in range(3)],
                )
                close(WITH_RIM)
                y = merge(0, CHUNK)
                target[block, 0:CHUNK, :] = y
                sums = tally(y.astype(F32), zeros())
                target[block, CHUNK:WITH_RIM, :] = (merge(CHUNK, 16).astype(F32) * chunk_mask).astype(BF16)
                for k in range(3):
                    packed = jnp.where(
                        tall == k * 4 + block, jnp.sum(sums[k], axis=0, keepdims=True), packed
                    )
        wide_out[t] = packed
        wide_in[t, rho] = packed
        for d in range(n_rng - 1):
            wide_copy(t, d, rho).start()

    def narrow(t):
        for d in range(n_rng - 1):
            wide_copy(t, d, peers[n_rng - 2 - d]).wait_recv()
        full = wide_in[t, 0]
        for other in range(1, n_rng):
            full = full + wide_in[t, other]
        part_out[t] = full
        part_in[t, quarter] = full
        for e in (2, 1, 3):
            part_copy(t, e, quarter).start()

    def finish(t):
        for e in (1, 3, 2):
            part_copy(t, e, behind[e]).wait_recv()
        full = part_in[t, 0]
        for other in range(1, QUARTERS):
            full = full + part_in[t, other]
        return factors(full[0:4], full[4:8], full[8:12])

    for e in (2, 1, 3):
        fac(e, behind[e]).wait_recv()
        split(e, behind[e]).wait_recv()
    for block in range(QUARTERS):
        stacked[block % 2, (block // 2) * WITH_RIM : (block // 2 + 1) * WITH_RIM, :] = rotate(
            split_in[block], fac_in[block, 0:1, :], fac_in[block, 1:2, :]
        )
    cross(0, middle_y)
    narrow(0)
    g_re, g_im = finish(0)

    for block in range(QUARTERS):
        stacked[block // 2, (block % 2) * WITH_RIM : (block % 2 + 1) * WITH_RIM, :] = rotate(
            middle_y[block], g_re[block : block + 1], g_im[block : block + 1]
        )
    cross(1, back_out)

    def back(e, slot):
        return copy_to(
            back_out.at[ahead[e]],
            back_in.at[slot],
            back_send.at[e - 1],
            back_recv.at[e - 1],
            (at_quarter(ahead[e]), rho),
        )

    def far(e):
        return copy_to(
            back_in.at[behind[e]], far_in.at[behind[e]], far_send.at[e], far_recv.at[e], (y_partner, rho)
        )

    back_in[quarter] = back_out[quarter]
    back(2, quarter).start()
    far(0).start()
    narrow(1)
    back(1, quarter).start()
    back(3, quarter).start()
    back(2, behind[2]).wait_recv()
    far(2).start()
    g_re, g_im = finish(1)
    mine_row = lax.broadcasted_iota(jnp.int32, (4, beams), 0) == quarter
    g_re = jnp.sum(jnp.where(mine_row, g_re, 0.0), axis=0, keepdims=True)
    g_im = jnp.sum(jnp.where(mine_row, g_im, 0.0), axis=0, keepdims=True)
    far_fac_out[...] = jnp.where(line == 0, g_re, jnp.where(line == 1, g_im, 0.0))
    far_fac = copy_to(far_fac_out, far_fac_in, far_send.at[4], far_recv.at[4], (y_partner, rho))
    far_fac.start()
    for e in (1, 3):
        back(e, behind[e]).wait_recv()
        far(e).start()

    core_copy(0).wait_send()
    core_copy(1).wait_send()

    def lay(source, target, re, im):
        for j in range(QUARTERS):
            target[j * CHUNK : (j + 1) * CHUNK, :] = rotate(source[j, 0:CHUNK, :], re, im)
        rim = jnp.concatenate(
            [
                source[QUARTERS - 1, CHUNK:WITH_RIM, :].astype(F32)[0:8],
                source[0, CHUNK:WITH_RIM, :].astype(F32)[8:16],
            ],
            axis=0,
        )
        target[rows:total, :] = rotate(rim, re, im)

    big = total // 3
    lay(back_in, own, g_re, g_im)

    @pl.loop(0, 3)
    def _(i):
        base = pl.multiple_of(i * big, 16)
        prod[pl.ds(base, big), :] = jnp.dot(own[pl.ds(base, big), :], matrix[10], preferred_element_type=F32)

    far_fac.wait_recv()
    for e in range(QUARTERS):
        copy_to(
            back_in.at[behind[e]], far_in.at[behind[e]], far_send.at[e], far_recv.at[e], (y_partner, rho)
        ).wait_recv()
    lay(far_in, got, far_fac_in[0:1, :], far_fac_in[1:2, :])
    y_mine = [taps[k, y_half, 3] for k in range(3)]
    y_theirs = [taps[k, 1 - y_half, 3] for k in range(3)]

    @pl.loop(0, 3)
    def _(i):
        base = pl.multiple_of(i * big, 16)
        theirs = jnp.dot(got[pl.ds(base, big), :], matrix[11], preferred_element_type=F32)
        spread(base, big, prod[pl.ds(base, big), :], theirs, y_mine, y_theirs)

    close(total)
    sums = zeros()
    for j in range(QUARTERS):
        y = merge(j * CHUNK, CHUNK)
        own[j * CHUNK : (j + 1) * CHUNK, :] = y
        sums = tally(y.astype(F32), sums)
    send_sums(1, sums)
    for j in range(QUARTERS):
        y = own[j * CHUNK : (j + 1) * CHUNK, :].astype(F32)
        for part in range(2):
            merged[part, :, j * CHUNK : (j + 1) * CHUNK] = y[:, part * beams : (part + 1) * beams].T.astype(
                BF16
            )
    g_re, g_im = take_sums(1)
    phase[0:1, :] = g_re
    phase[1:2, :] = g_im

    for s in range(2):
        for d in range(n_rng - 1):
            sums_copy(s, d, rho).wait_send()
            wide_copy(s, d, rho).wait_send()
        for e in range(1, QUARTERS):
            part_copy(s, e, quarter).wait_send()
    for e in range(1, QUARTERS):
        split(e, quarter).wait_send()
        fac(e, quarter).wait_send()
        back(e, quarter).wait_send()
    for e in range(QUARTERS):
        far(e).wait_send()
    far_fac.wait_send()


def solution(mesh):
    n_rng = mesh.shape["rng"]

    def on_device(image, stencil, interp_weights, range_taps):
        _, beams, rows = image.shape
        total = rows + 16
        cosines, sines = angle_tables(beams)
        hbm = pl.BlockSpec(memory_space=pltpu.HBM)
        vmem = pl.BlockSpec(memory_space=pltpu.VMEM)
        smem = pl.BlockSpec(memory_space=pltpu.SMEM)
        dma = pltpu.SemaphoreType.DMA
        return pl.pallas_call(
            functools.partial(kernel, n_rng),
            out_shape=(
                jax.ShapeDtypeStruct((2, beams, rows), BF16),
                jax.ShapeDtypeStruct((2, beams), F32),
            ),
            in_specs=[smem, smem, hbm, hbm, hbm],
            out_specs=(vmem, vmem),
            scratch_shapes=[
                pltpu.VMEM((2, beams, rows), BF16),
                pltpu.VMEM((SECTIONS * 4, TAPS, beams), jnp.int32),
                pltpu.VMEM((2, SECTIONS * 4, beams), F32),
                pltpu.VMEM((total, 2 * beams), BF16),
                pltpu.VMEM((total, 2 * beams), BF16),
                pltpu.VMEM((12, 2 * beams, 2 * beams), BF16),
                pltpu.VMEM((total + 8, 2 * beams), F32),
                pltpu.VMEM((total, 2 * beams), F32),
                pltpu.VMEM((total + 8, 2 * beams), F32),
                pltpu.VMEM((total, 2 * beams), F32),
                pltpu.VMEM((16, 2 * beams), BF16),
                pltpu.VMEM((2, 16, 2 * beams), BF16),
                pltpu.VMEM((2, 8, beams), F32),
                pltpu.VMEM((2, n_rng, 8, beams), F32),
                pltpu.VMEM((QUARTERS, WITH_RIM, 2 * beams), BF16),
                pltpu.VMEM((QUARTERS, WITH_RIM, 2 * beams), BF16),
                pltpu.VMEM((2, 2 * WITH_RIM, 2 * beams), BF16),
                pltpu.VMEM((2, 2 * WITH_RIM, 2 * beams), F32),
                pltpu.VMEM((QUARTERS, WITH_RIM, 2 * beams), BF16),
                pltpu.VMEM((QUARTERS, WITH_RIM, 2 * beams), BF16),
                pltpu.VMEM((QUARTERS, WITH_RIM, 2 * beams), BF16),
                pltpu.VMEM((QUARTERS, WITH_RIM, 2 * beams), BF16),
                pltpu.VMEM((8, beams), F32),
                pltpu.VMEM((QUARTERS, 8, beams), F32),
                pltpu.VMEM((8, beams), F32),
                pltpu.VMEM((8, beams), F32),
                pltpu.VMEM((2, 16, beams), F32),
                pltpu.VMEM((2, n_rng, 16, beams), F32),
                pltpu.VMEM((2, 16, beams), F32),
                pltpu.VMEM((2, QUARTERS, 16, beams), F32),
                dma((3,)),
                dma((2,)),
                dma((2,)),
                dma((2,)),
                dma((2,)),
                dma((2, n_rng - 1)),
                dma((2, n_rng - 1)),
                dma((QUARTERS - 1,)),
                dma((QUARTERS - 1,)),
                dma((QUARTERS - 1,)),
                dma((QUARTERS - 1,)),
                dma((QUARTERS + 1,)),
                dma((QUARTERS + 1,)),
                dma((QUARTERS - 1,)),
                dma((QUARTERS - 1,)),
                dma((2, n_rng - 1)),
                dma((2, n_rng - 1)),
                dma((2, QUARTERS - 1)),
                dma((2, QUARTERS - 1)),
            ],
            compiler_params=pltpu.CompilerParams(
                collective_id=0, has_side_effects=True, vmem_limit_bytes=67043328
            ),
        )(
            interp_weights,
            range_taps.transpose(2, 1, 0),
            image,
            stencil.transpose(0, 1, 2, 4, 3).reshape(SECTIONS * 4, TAPS, beams),
            jnp.asarray(np.stack([cosines, sines])),
        )

    return jax.shard_map(
        on_device,
        mesh=mesh,
        in_specs=(P(None, "sub", "rng"), P(), P(), P()),
        out_specs=(P(None, "sub", "rng"), P(None, "sub")),
        check_vma=False,
    )
```

time: 88.7 us -> 79.4 us (0.90)
  Pallas kernels: 84.9 us -> 76.2 us
    pallas_call x1, Pallas kernels: 84.9 us -> 76.2 us  [on_device(): pl.pallas_call(functools.partial(kernel, n_rng), out_shape=(jax.ShapeDtyp...]
where the time goes in v3:
time: 79.4 us; the launch traced here: 79.3 us
  Pallas kernels  76.2 us (96%)
  local copies, waits for them, and re-layouts  2.45 us (3%)
    pallas_call x1, Pallas kernels, on_device(): pl.pallas_call(functools.partial(kernel, n_rng), out_shape=(jax.ShapeDtyp...  76.2 us
    unnamed x4, local copies, waits for them, and re-layouts  2.45 us

profile of v3, /device:TPU:16, one launch (start us, length us, event | category | flops | bytes accessed | tf_op | source)
XLA Modules:
  0.0 79.3 jit_solution(1033513111330387382)
XLA Ops:
  0.6 76.2 %shard_map.68 = (bf16[2,256,512]{2,1,0:T(8,128)(2,1)}, f32[2,256]{1,0:T(2,128)}) custom-call(f32[4,4]{1,0:T(4,128)} %weights.1, f32[3,2,4]{2,1,0:T(2,128)} %bitcast.5, bf16[2,256,512]{2,1,0:T(8,128)(2,1)} %image_hbm.1, s32[16,4,256]{2,1,0:T(4,128)} %bitcast.4, f32[2,16,256]{2,1,0:T(8,128)} %constant.2.clone.trig_hbm), custom_call_target="tpu_custom_call" | custom-call | tf_op jit(solution)/shard_map/pallas_call | solution.py:526
  76.8 0.0 copy-start
  76.8 1.9 %copy.9 = bf16[2,256,512]{2,1,0:T(8,128)(2,1)} copy(bf16[2,256,512]{2,1,0:T(8,128)(2,1)} %get-tuple-element.4) | data formatting | bytes 1048576
  78.7 0.0 copy-done
  78.7 0.6 copy.10
Async XLA Ops:
  76.8 1.9 %copy-start = (f32[2,256]{1,0:T(2,128)S(1)}, f32[2,256]{1,0:T(2,128)}, u32[]{:S(2)}) copy-start(f32[2,256]{1,0:T(2,128)} %get-tuple-element.5) | copy-start | bytes 6148

commit v4 on v3

--- a/solution.py
+++ b/solution.py
@@ -14,6 +14,8 @@
 QUARTERS = 4
 CHUNK = 128
 WITH_RIM = CHUNK + 16
+PARTS = ((0, CHUNK // 2), (CHUNK // 2, CHUNK // 2), (CHUNK, 16))
+RIM = 2
 MESH = pl.DeviceIdType.MESH
 F32 = jnp.float32
 BF16 = jnp.bfloat16
@@ -392,11 +394,13 @@
             full = full + part_in[t, other]
         return factors(full[0:4], full[4:8], full[8:12])
 
-    for e in (2, 1, 3):
-        fac(e, behind[e]).wait_recv()
-        split(e, behind[e]).wait_recv()
-    for block in range(QUARTERS):
-        stacked[block % 2, (block // 2) * WITH_RIM : (block // 2 + 1) * WITH_RIM, :] = rotate(
+    for e in (0, 2, 1, 3):
+        block = behind[e]
+        if e > 0:
+            fac(e, block).wait_recv()
+            split(e, block).wait_recv()
+        base = pl.multiple_of(block // 2 * WITH_RIM, 16)
+        stacked[lax.rem(block, 2), pl.ds(base, WITH_RIM), :] = rotate(
             split_in[block], fac_in[block, 0:1, :], fac_in[block, 1:2, :]
         )
     cross(0, middle_y)
@@ -409,45 +413,62 @@
         )
     cross(1, back_out)
 
-    def back(e, slot):
-        return copy_to(
-            back_out.at[ahead[e]],
-            back_in.at[slot],
-            back_send.at[e - 1],
-            back_recv.at[e - 1],
+    def ends(slot):
+        return lax.rem(slot, QUARTERS - 1) == 0
+
+    def each(slot, action):
+        pl.when(ends(slot))(lambda: action(RIM))
+        action(0)
+        action(1)
+
+    def back(e, slot, k):
+        rows_k = pl.ds(*PARTS[k])
+        return copy_to(
+            back_out.at[ahead[e], rows_k],
+            back_in.at[slot, rows_k],
+            back_send.at[e - 1, k],
+            back_recv.at[e - 1, k],
             (at_quarter(ahead[e]), rho),
         )
 
-    def far(e):
-        return copy_to(
-            back_in.at[behind[e]], far_in.at[behind[e]], far_send.at[e], far_recv.at[e], (y_partner, rho)
-        )
+    def far(e, k):
+        rows_k = pl.ds(*PARTS[k])
+        return copy_to(
+            back_in.at[behind[e], rows_k],
+            far_in.at[behind[e], rows_k],
+            far_send.at[e, k],
+            far_recv.at[e, k],
+            (y_partner, rho),
+        )
+
+    def pass_on(e):
+        def action(k):
+            back(e, behind[e], k).wait_recv()
+            far(e, k).start()
+
+        each(behind[e], action)
 
     back_in[quarter] = back_out[quarter]
-    back(2, quarter).start()
-    far(0).start()
+    for e in (1, 3):
+        each(quarter, lambda k, e=e: back(e, quarter, k).start())
+    each(quarter, lambda k: far(0, k).start())
     narrow(1)
-    back(1, quarter).start()
-    back(3, quarter).start()
-    back(2, behind[2]).wait_recv()
-    far(2).start()
+    each(quarter, lambda k: back(2, quarter, k).start())
+    for e in (1, 3):
+        pass_on(e)
     g_re, g_im = finish(1)
     mine_row = lax.broadcasted_iota(jnp.int32, (4, beams), 0) == quarter
     g_re = jnp.sum(jnp.where(mine_row, g_re, 0.0), axis=0, keepdims=True)
     g_im = jnp.sum(jnp.where(mine_row, g_im, 0.0), axis=0, keepdims=True)
     far_fac_out[...] = jnp.where(line == 0, g_re, jnp.where(line == 1, g_im, 0.0))
-    far_fac = copy_to(far_fac_out, far_fac_in, far_send.at[4], far_recv.at[4], (y_partner, rho))
+    far_fac = copy_to(far_fac_out, far_fac_in, far_send.at[4, 0], far_recv.at[4, 0], (y_partner, rho))
     far_fac.start()
-    for e in (1, 3):
-        back(e, behind[e]).wait_recv()
-        far(e).start()
+    pass_on(2)
 
     core_copy(0).wait_send()
     core_copy(1).wait_send()
 
-    def lay(source, target, re, im):
-        for j in range(QUARTERS):
-            target[j * CHUNK : (j + 1) * CHUNK, :] = rotate(source[j, 0:CHUNK, :], re, im)
+    def rim_of(source, re, im):
         rim = jnp.concatenate(
             [
                 source[QUARTERS - 1, CHUNK:WITH_RIM, :].astype(F32)[0:8],
@@ -455,10 +476,12 @@
             ],
             axis=0,
         )
-        target[rows:total, :] = rotate(rim, re, im)
-
+        return rotate(rim, re, im)
+
+    for j in range(QUARTERS):
+        own[j * CHUNK : (j + 1) * CHUNK, :] = rotate(back_in[j, 0:CHUNK, :], g_re, g_im)
+    own[rows:total, :] = rim_of(back_in, g_re, g_im)
     big = total // 3
-    lay(back_in, own, g_re, g_im)
 
     @pl.loop(0, 3)
     def _(i):
@@ -466,20 +489,18 @@
         prod[pl.ds(base, big), :] = jnp.dot(own[pl.ds(base, big), :], matrix[10], preferred_element_type=F32)
 
     far_fac.wait_recv()
-    for e in range(QUARTERS):
-        copy_to(
-            back_in.at[behind[e]], far_in.at[behind[e]], far_send.at[e], far_recv.at[e], (y_partner, rho)
-        ).wait_recv()
-    lay(far_in, got, far_fac_in[0:1, :], far_fac_in[1:2, :])
+    far_re, far_im = far_fac_in[0:1, :], far_fac_in[1:2, :]
     y_mine = [taps[k, y_half, 3] for k in range(3)]
     y_theirs = [taps[k, 1 - y_half, 3] for k in range(3)]
-
-    @pl.loop(0, 3)
-    def _(i):
-        base = pl.multiple_of(i * big, 16)
-        theirs = jnp.dot(got[pl.ds(base, big), :], matrix[11], preferred_element_type=F32)
-        spread(base, big, prod[pl.ds(base, big), :], theirs, y_mine, y_theirs)
-
+    for e in (0, 1, 3, 2):
+        each(behind[e], lambda k, e=e: far(e, k).wait_recv())
+        base = pl.multiple_of(behind[e] * CHUNK, CHUNK)
+        theirs = jnp.dot(
+            rotate(far_in[behind[e], 0:CHUNK, :], far_re, far_im), matrix[11], preferred_element_type=F32
+        )
+        spread(base, CHUNK, prod[pl.ds(base, CHUNK), :], theirs, y_mine, y_theirs)
+    theirs = jnp.dot(rim_of(far_in, far_re, far_im), matrix[11], preferred_element_type=F32)
+    spread(rows, 16, prod[rows:total, :], theirs, y_mine, y_theirs)
     close(total)
     sums = zeros()
     for j in range(QUARTERS):
@@ -506,9 +527,9 @@
     for e in range(1, QUARTERS):
         split(e, quarter).wait_send()
         fac(e, quarter).wait_send()
-        back(e, quarter).wait_send()
+        each(quarter, lambda k, e=e: back(e, quarter, k).wait_send())
     for e in range(QUARTERS):
-        far(e).wait_send()
+        each(behind[e], lambda k, e=e: far(e, k).wait_send())
     far_fac.wait_send()
 
 
@@ -571,10 +592,10 @@
                 dma((2, n_rng - 1)),
                 dma((QUARTERS - 1,)),
                 dma((QUARTERS - 1,)),
-                dma((QUARTERS - 1,)),
-                dma((QUARTERS - 1,)),
-                dma((QUARTERS + 1,)),
-                dma((QUARTERS + 1,)),
+                dma((QUARTERS - 1, 3)),
+                dma((QUARTERS - 1, 3)),
+                dma((QUARTERS + 1, 3)),
+                dma((QUARTERS + 1, 3)),
                 dma((QUARTERS - 1,)),
                 dma((QUARTERS - 1,)),
                 dma((2, n_rng - 1)),

time: 79.4 us -> 74.7 us (0.941)
  Pallas kernels: 76.2 us -> 71.5 us
    pallas_call x1, Pallas kernels: 76.2 us -> 71.5 us  [on_device(): pl.pallas_call(functools.partial(kernel, n_rng), out_shape=(jax.ShapeDtyp...]
where the time goes in v4:
time: 74.7 us; the launch traced here: 74.6 us
  Pallas kernels  71.5 us (96%)
  local copies, waits for them, and re-layouts  2.45 us (3%)
    pallas_call x1, Pallas kernels, on_device(): pl.pallas_call(functools.partial(kernel, n_rng), out_shape=(jax.ShapeDtyp...  71.5 us
    unnamed x4, local copies, waits for them, and re-layouts  2.45 us

profile of v4, /device:TPU:16, one launch (start us, length us, event | category | flops | bytes accessed | tf_op | source)
XLA Modules:
  0.0 74.6 jit_solution(9587730989417801889)
XLA Ops:
  0.6 71.5 %shard_map.68 = (bf16[2,256,512]{2,1,0:T(8,128)(2,1)}, f32[2,256]{1,0:T(2,128)}) custom-call(f32[4,4]{1,0:T(4,128)} %weights.1, f32[3,2,4]{2,1,0:T(2,128)} %bitcast.5, bf16[2,256,512]{2,1,0:T(8,128)(2,1)} %image_hbm.1, s32[16,4,256]{2,1,0:T(4,128)} %bitcast.4, f32[2,16,256]{2,1,0:T(8,128)} %constant.2.clone.trig_hbm), custom_call_target="tpu_custom_call" | custom-call | tf_op jit(solution)/shard_map/pallas_call | solution.py:547
  72.1 0.0 copy-start
  72.1 1.9 %copy.9 = bf16[2,256,512]{2,1,0:T(8,128)(2,1)} copy(bf16[2,256,512]{2,1,0:T(8,128)(2,1)} %get-tuple-element.4) | data formatting | bytes 1048576
  74.0 0.0 copy-done
  74.0 0.6 copy.10
Async XLA Ops:
  72.1 1.9 %copy-start = (f32[2,256]{1,0:T(2,128)S(1)}, f32[2,256]{1,0:T(2,128)}, u32[]{:S(2)}) copy-start(f32[2,256]{1,0:T(2,128)} %get-tuple-element.5) | copy-start | bytes 6148

commit v5 on v4

--- a/solution.py
+++ b/solution.py
@@ -39,7 +39,7 @@
     image_hbm,
     stencil_hbm,
     trig_hbm,
-    merged,
+    merged_hbm,
     phase,
     image,
     stencil,
@@ -114,6 +114,9 @@
         pl.semaphore_signal(barrier, inc=1, device_id=(other, rho), device_id_type=MESH)
     for peer in peers:
         pl.semaphore_signal(barrier, inc=1, device_id=(sub, peer), device_id_type=MESH)
+    below, above = lax.rem(rho + n_rng - 1, n_rng), lax.rem(rho + 1, n_rng)
+    for peer in (below, above):
+        pl.semaphore_signal(barrier, inc=1, device_id=(core_partner, peer), device_id_type=MESH)
 
     loads = [
         pltpu.make_async_copy(image_hbm, image, load_sem.at[0]),
@@ -156,24 +159,25 @@
     build(0, 0, core_half, core_half)
     build(1, 0, core_half, 1 - core_half)
 
-    pl.semaphore_wait(barrier, 1 + 1 + QUARTERS - 1 + n_rng - 1)
-
-    def core_copy(rim):
-        base, size = (rows, 16) if rim else (0, rows)
-        return copy_to(
-            own.at[pl.ds(base, size)], got.at[pl.ds(base, size)], core_send.at[rim], core_recv.at[rim], (core_partner, rho)
-        )
-
-    below, above = lax.rem(rho + n_rng - 1, n_rng), lax.rem(rho + 1, n_rng)
-
-    def edge(side):
-        return copy_to(
-            edge_out, edge_in.at[side], edge_send.at[side], edge_recv.at[side], (sub, above if side == 0 else below)
-        )
-
-    edge(0).start()
-    edge(1).start()
-    core_copy(0).start()
+    pl.semaphore_wait(barrier, 1 + 1 + QUARTERS - 1 + n_rng - 1 + 2)
+
+    core_copy = copy_to(
+        own.at[pl.ds(0, rows)], got.at[pl.ds(0, rows)], core_send.at[0], core_recv.at[0], (core_partner, rho)
+    )
+
+    def edge(whose, side):
+        return copy_to(
+            edge_out,
+            edge_in.at[whose, side],
+            edge_send.at[whose, side],
+            edge_recv.at[whose, side],
+            (core_partner if whose else sub, above if side == 0 else below),
+        )
+
+    for whose in range(2):
+        for side in range(2):
+            edge(whose, side).start()
+    core_copy.start()
 
     row_id = lax.broadcasted_iota(jnp.int32, (16, width), 0)
     one = jnp.float32(1.0)
@@ -259,7 +263,7 @@
 
     core_mine = [taps[k, core_half, 0] for k in range(3)]
     core_theirs = [taps[k, 1 - core_half, 0] for k in range(3)]
-    core_copy(0).wait_recv()
+    core_copy.wait_recv()
 
     @pl.loop(0, 2)
     def _(i):
@@ -267,24 +271,32 @@
         theirs = jnp.dot(got[pl.ds(base, half_rows), :], matrix[1], preferred_element_type=F32)
         spread(base, half_rows, prod[pl.ds(base, half_rows), :], theirs, core_mine, core_theirs)
 
-    edge(0).wait()
-    edge(1).wait()
-    halo = jnp.concatenate([edge_in[1].astype(F32)[0:8], edge_in[0].astype(F32)[8:16]], axis=0)
-    own[rows:total, :] = (halo * mask).astype(BF16)
-    core_copy(1).start()
-    mine = jnp.dot(own[rows:total, :], matrix[0], preferred_element_type=F32)
-    core_copy(1).wait_recv()
-    theirs = jnp.dot(got[rows:total, :], matrix[1], preferred_element_type=F32)
-    spread(rows, 16, mine, theirs, core_mine, core_theirs)
-    close(total)
     sums = zeros()
-    for j in range(QUARTERS):
+
+    def settle(j, sums):
         y = merge(j * CHUNK, CHUNK)
         split_out[j, 0:CHUNK, :] = y
         y = y.astype(F32)
-        sums = tally(y, sums)
         prod[j * CHUNK : j * CHUNK + 8, :] = y[0:8]
         prod[(j + 1) * CHUNK - 8 : (j + 1) * CHUNK, :] = y[CHUNK - 8 : CHUNK]
+        return tally(y, sums)
+
+    for j in range(1, QUARTERS - 1):
+        sums = settle(j, sums)
+    rims = []
+    for whose in range(2):
+        edge(whose, 0).wait()
+        edge(whose, 1).wait()
+        halo = jnp.concatenate(
+            [edge_in[whose, 1].astype(F32)[0:8], edge_in[whose, 0].astype(F32)[8:16]], axis=0
+        )
+        rims.append(
+            jnp.dot((halo * mask).astype(BF16), matrix[whose], preferred_element_type=F32)
+        )
+    spread(rows, 16, rims[0], rims[1], core_mine, core_theirs)
+    close(total)
+    for j in (0, QUARTERS - 1):
+        sums = settle(j, sums)
     send_sums(0, sums)
     prod[rows:total, :] = merge(rows, 16).astype(F32) * mask
     for j in range(QUARTERS):
@@ -309,6 +321,7 @@
         )
 
     split(2, quarter).start()
+    split(1, quarter).start()
     split_in[quarter] = split_out[quarter]
     g_re, g_im = take_sums(0)
     packed = jnp.where(line == 0, g_re, jnp.where(line == 1, g_im, 0.0))
@@ -316,7 +329,6 @@
     fac_in[quarter] = packed
     for e in (1, 3, 2):
         fac(e, quarter).start()
-    split(1, quarter).start()
     split(3, quarter).start()
 
     for half in range(2):
@@ -465,8 +477,7 @@
     far_fac.start()
     pass_on(2)
 
-    core_copy(0).wait_send()
-    core_copy(1).wait_send()
+    core_copy.wait_send()
 
     def rim_of(source, re, im):
         rim = jnp.concatenate(
@@ -511,9 +522,11 @@
     for j in range(QUARTERS):
         y = own[j * CHUNK : (j + 1) * CHUNK, :].astype(F32)
         for part in range(2):
-            merged[part, :, j * CHUNK : (j + 1) * CHUNK] = y[:, part * beams : (part + 1) * beams].T.astype(
+            image[part, :, j * CHUNK : (j + 1) * CHUNK] = y[:, part * beams : (part + 1) * beams].T.astype(
                 BF16
             )
+    out = pltpu.make_async_copy(image, merged_hbm, load_sem.at[0])
+    out.start()
     g_re, g_im = take_sums(1)
     phase[0:1, :] = g_re
     phase[1:2, :] = g_im
@@ -531,6 +544,7 @@
     for e in range(QUARTERS):
         each(behind[e], lambda k, e=e: far(e, k).wait_send())
     far_fac.wait_send()
+    out.wait()
 
 
 def solution(mesh):
@@ -551,7 +565,7 @@
                 jax.ShapeDtypeStruct((2, beams), F32),
             ),
             in_specs=[smem, smem, hbm, hbm, hbm],
-            out_specs=(vmem, vmem),
+            out_specs=(hbm, vmem),
             scratch_shapes=[
                 pltpu.VMEM((2, beams, rows), BF16),
                 pltpu.VMEM((SECTIONS * 4, TAPS, beams), jnp.int32),
@@ -564,7 +578,7 @@
                 pltpu.VMEM((total + 8, 2 * beams), F32),
                 pltpu.VMEM((total, 2 * beams), F32),
                 pltpu.VMEM((16, 2 * beams), BF16),
-                pltpu.VMEM((2, 16, 2 * beams), BF16),
+                pltpu.VMEM((2, 2, 16, 2 * beams), BF16),
                 pltpu.VMEM((2, 8, beams), F32),
                 pltpu.VMEM((2, n_rng, 8, beams), F32),
                 pltpu.VMEM((QUARTERS, WITH_RIM, 2 * beams), BF16),
@@ -584,10 +598,10 @@
                 pltpu.VMEM((2, 16, beams), F32),
                 pltpu.VMEM((2, QUARTERS, 16, beams), F32),
                 dma((3,)),
-                dma((2,)),
-                dma((2,)),
-                dma((2,)),
-                dma((2,)),
+                dma((1,)),
+                dma((1,)),
+                dma((2, 2)),
+                dma((2, 2)),
                 dma((2, n_rng - 1)),
                 dma((2, n_rng - 1)),
                 dma((QUARTERS - 1,)),

time: 74.7 us -> 72.8 us (0.975)
  Pallas kernels: 71.5 us -> 69.6 us
    pallas_call x1, Pallas kernels: 71.5 us -> 69.6 us  [on_device(): pl.pallas_call(functools.partial(kernel, n_rng), out_shape=(jax.ShapeDtyp...]
where the time goes in v5:
time: 72.8 us; the launch traced here: 72.7 us
  Pallas kernels  69.6 us (96%)
  local copies, waits for them, and re-layouts  2.45 us (3%)
    pallas_call x1, Pallas kernels, on_device(): pl.pallas_call(functools.partial(kernel, n_rng), out_shape=(jax.ShapeDtyp...  69.6 us
    unnamed x4, local copies, waits for them, and re-layouts  2.45 us

profile of v5, /device:TPU:16, one launch (start us, length us, event | category | flops | bytes accessed | tf_op | source)
XLA Modules:
  0.0 72.7 jit_solution(17315209505790154506)
XLA Ops:
  0.6 69.6 %shard_map.68 = (bf16[2,256,512]{2,1,0:T(8,128)(2,1)}, f32[2,256]{1,0:T(2,128)}) custom-call(f32[4,4]{1,0:T(4,128)} %weights.1, f32[3,2,4]{2,1,0:T(2,128)} %bitcast.5, bf16[2,256,512]{2,1,0:T(8,128)(2,1)} %image_hbm.1, s32[16,4,256]{2,1,0:T(4,128)} %bitcast.4, f32[2,16,256]{2,1,0:T(8,128)} %constant.2.clone.trig_hbm), custom_call_target="tpu_custom_call" | custom-call | tf_op jit(solution)/shard_map/pallas_call | solution.py:561
  70.2 0.0 copy-start
  70.2 1.9 %copy.9 = bf16[2,256,512]{2,1,0:T(8,128)(2,1)} copy(bf16[2,256,512]{2,1,0:T(8,128)(2,1)} %get-tuple-element.4) | data formatting | bytes 1048576
  72.1 0.0 copy-done
  72.1 0.6 copy.10
Async XLA Ops:
  70.2 1.9 %copy-start = (f32[2,256]{1,0:T(2,128)S(1)}, f32[2,256]{1,0:T(2,128)}, u32[]{:S(2)}) copy-start(f32[2,256]{1,0:T(2,128)} %get-tuple-element.5) | copy-start | bytes 6148

commit v6 on v5

--- a/solution.py
+++ b/solution.py
@@ -352,11 +352,12 @@
             (at_quarter(ahead[e]), rho),
         )
 
-    tall = lax.broadcasted_iota(jnp.int32, (16, beams), 0)
+    lanes = beams // 2
+    tall = lax.broadcasted_iota(jnp.int32, (24, lanes), 0)
 
     def cross(t, target):
         s = t + 1
-        packed = jnp.zeros((16, beams), F32)
+        packed = jnp.zeros((24, lanes), F32)
         for half in range(2):
             for child in range(2):
                 terms[child] = jnp.dot(
@@ -379,9 +380,13 @@
                 sums = tally(y.astype(F32), zeros())
                 target[block, CHUNK:WITH_RIM, :] = (merge(CHUNK, 16).astype(F32) * chunk_mask).astype(BF16)
                 for k in range(3):
-                    packed = jnp.where(
-                        tall == k * 4 + block, jnp.sum(sums[k], axis=0, keepdims=True), packed
-                    )
+                    value = jnp.sum(sums[k], axis=0, keepdims=True)
+                    for side in range(2):
+                        packed = jnp.where(
+                            tall == k * 8 + side * 4 + block,
+                            value[:, side * lanes : (side + 1) * lanes],
+                            packed,
+                        )
         wide_out[t] = packed
         wide_in[t, rho] = packed
         for d in range(n_rng - 1):
@@ -404,7 +409,8 @@
         full = part_in[t, 0]
         for other in range(1, QUARTERS):
             full = full + part_in[t, other]
-        return factors(full[0:4], full[4:8], full[8:12])
+        whole = [jnp.concatenate([full[k : k + 4], full[k + 4 : k + 8]], axis=1) for k in (0, 8, 16)]
+        return factors(*whole)
 
     for e in (0, 2, 1, 3):
         block = behind[e]
@@ -593,10 +599,10 @@
                 pltpu.VMEM((QUARTERS, 8, beams), F32),
                 pltpu.VMEM((8, beams), F32),
                 pltpu.VMEM((8, beams), F32),
-                pltpu.VMEM((2, 16, beams), F32),
-                pltpu.VMEM((2, n_rng, 16, beams), F32),
-                pltpu.VMEM((2, 16, beams), F32),
-                pltpu.VMEM((2, QUARTERS, 16, beams), F32),
+                pltpu.VMEM((2, 24, beams // 2), F32),
+                pltpu.VMEM((2, n_rng, 24, beams // 2), F32),
+                pltpu.VMEM((2, 24, beams // 2), F32),
+                pltpu.VMEM((2, QUARTERS, 24, beams // 2), F32),
                 dma((3,)),
                 dma((1,)),
                 dma((1,)),

time: 72.8 us -> 72.2 us (level)
  no operation moved by 1% of the time
where the time goes in v6:
time: 72.2 us; the launch traced here: 72 us
  Pallas kernels  68.9 us (95%)
  local copies, waits for them, and re-layouts  2.45 us (3%)
    pallas_call x1, Pallas kernels, on_device(): pl.pallas_call(functools.partial(kernel, n_rng), out_shape=(jax.ShapeDtyp...  68.9 us
    unnamed x4, local copies, waits for them, and re-layouts  2.45 us

profile of v6, /device:TPU:16, one launch (start us, length us, event | category | flops | bytes accessed | tf_op | source)
XLA Modules:
  0.0 72.0 jit_solution(18282267808709845989)
XLA Ops:
  0.6 68.9 %shard_map.68 = (bf16[2,256,512]{2,1,0:T(8,128)(2,1)}, f32[2,256]{1,0:T(2,128)}) custom-call(f32[4,4]{1,0:T(4,128)} %weights.1, f32[3,2,4]{2,1,0:T(2,128)} %bitcast.5, bf16[2,256,512]{2,1,0:T(8,128)(2,1)} %image_hbm.1, s32[16,4,256]{2,1,0:T(4,128)} %bitcast.4, f32[2,16,256]{2,1,0:T(8,128)} %constant.2.clone.trig_hbm), custom_call_target="tpu_custom_call" | custom-call | tf_op jit(solution)/shard_map/pallas_call | solution.py:567
  69.6 0.0 copy-start
  69.6 1.9 %copy.9 = bf16[2,256,512]{2,1,0:T(8,128)(2,1)} copy(bf16[2,256,512]{2,1,0:T(8,128)(2,1)} %get-tuple-element.4) | data formatting | bytes 1048576
  71.4 0.0 copy-done
  71.4 0.6 copy.10
Async XLA Ops:
  69.6 1.9 %copy-start = (f32[2,256]{1,0:T(2,128)S(1)}, f32[2,256]{1,0:T(2,128)}, u32[]{:S(2)}) copy-start(f32[2,256]{1,0:T(2,128)} %get-tuple-element.5) | copy-start | bytes 6148

commit v7 on v6

--- a/solution.py
+++ b/solution.py
@@ -156,8 +156,6 @@
     low_edge = own[0:16, :].astype(F32)
     high_edge = own[rows - 16 : rows, :].astype(F32)
     edge_out[...] = jnp.concatenate([low_edge[0:8], high_edge[8:16]], axis=0).astype(BF16)
-    build(0, 0, core_half, core_half)
-    build(1, 0, core_half, 1 - core_half)
 
     pl.semaphore_wait(barrier, 1 + 1 + QUARTERS - 1 + n_rng - 1 + 2)
 
@@ -178,6 +176,8 @@
         for side in range(2):
             edge(whose, side).start()
     core_copy.start()
+    build(0, 0, core_half, core_half)
+    build(1, 0, core_half, 1 - core_half)
 
     row_id = lax.broadcasted_iota(jnp.int32, (16, width), 0)
     one = jnp.float32(1.0)

time: 72.2 us -> 72.2 us (level)
  no operation moved by 1% of the time
where the time goes in v7:
time: 72.2 us; the launch traced here: 72 us
  Pallas kernels  68.9 us (95%)
  local copies, waits for them, and re-layouts  2.45 us (3%)
    pallas_call x1, Pallas kernels, on_device(): pl.pallas_call(functools.partial(kernel, n_rng), out_shape=(jax.ShapeDtyp...  68.9 us
    unnamed x4, local copies, waits for them, and re-layouts  2.45 us

profile of v7, /device:TPU:16, one launch (start us, length us, event | category | flops | bytes accessed | tf_op | source)
XLA Modules:
  0.0 72.0 jit_solution(5300491436461788938)
XLA Ops:
  0.6 68.9 %shard_map.68 = (bf16[2,256,512]{2,1,0:T(8,128)(2,1)}, f32[2,256]{1,0:T(2,128)}) custom-call(f32[4,4]{1,0:T(4,128)} %weights.1, f32[3,2,4]{2,1,0:T(2,128)} %bitcast.5, bf16[2,256,512]{2,1,0:T(8,128)(2,1)} %image_hbm.1, s32[16,4,256]{2,1,0:T(4,128)} %bitcast.4, f32[2,16,256]{2,1,0:T(8,128)} %constant.2.clone.trig_hbm), custom_call_target="tpu_custom_call" | custom-call | tf_op jit(solution)/shard_map/pallas_call | solution.py:567
  69.6 0.0 copy-start
  69.6 1.9 %copy.9 = bf16[2,256,512]{2,1,0:T(8,128)(2,1)} copy(bf16[2,256,512]{2,1,0:T(8,128)(2,1)} %get-tuple-element.4) | data formatting | bytes 1048576
  71.5 0.0 copy-done
  71.5 0.6 copy.10
Async XLA Ops:
  69.6 1.9 %copy-start = (f32[2,256]{1,0:T(2,128)S(1)}, f32[2,256]{1,0:T(2,128)}, u32[]{:S(2)}) copy-start(f32[2,256]{1,0:T(2,128)} %get-tuple-element.5) | copy-start | bytes 6148
